TPU v7x, 16 devices: a whole 2x2x2 slice. The times are simulated.
16 devices in a mesh: dp: 1, tp: 16 (over x, y, z, core).
Axes of the slice: x: 2, y: 2, z: 2, core: 2. Of those that a mesh axis runs over, the one named last changes fastest.
Arguments:
- x: bfloat16 [2560, 7168], P(('dp', 'tp'))
- dy: bfloat16 [2560, 7168], P(('dp', 'tp'))
- gate: bfloat16 [2560, 18432], P('dp', 'tp')
- up: bfloat16 [2560, 18432], P('dp', 'tp')
- w_gate: bfloat16 [7168, 18432], P(None, 'tp')
- w_up: bfloat16 [7168, 18432], P(None, 'tp')
- w_down: bfloat16 [18432, 7168], P('tp')
Outputs:
- output 1: bfloat16 [2560, 7168], P(('dp', 'tp'))
- output 2: bfloat16 [7168, 18432], P('dp', 'tp')
- output 3: bfloat16 [7168, 18432], P('dp', 'tp')
- output 4: bfloat16 [18432, 7168], P(('dp', 'tp'))
All inputs are finite; a program needn't handle non-finite values.
Results may differ from a plain program's by a relative error of at most 0.012.
Values are sent between devices in bfloat16 or wider.
A program may use at most 2 GiB of HBM per device.

v0:
```python
import jax
import jax.numpy as jnp


def act(gate, up):
    return jax.nn.silu(gate) * up


def solution(mesh):
    def step(x, dy, gate, up, w_gate, w_up, w_down):
        hidden, back = jax.vjp(act, gate.astype(jnp.float32), up.astype(jnp.float32))
        d_hidden = jnp.dot(dy, w_down.T, preferred_element_type=jnp.float32)
        d_gate, d_up = (g.astype(jnp.bfloat16) for g in back(d_hidden))
        dx = jnp.dot(d_gate, w_gate.T) + jnp.dot(d_up, w_up.T)
        groups = mesh.shape["dp"]

        def by_group(a, b):
            a, b = (t.reshape(groups, -1, t.shape[-1]) for t in (a, b))
            product = jnp.einsum("gta,gtb->gab", a, b, preferred_element_type=jnp.float32)
            return product.astype(jnp.bfloat16).reshape(-1, b.shape[-1])

        return dx, by_group(x, d_gate), by_group(x, d_up), by_group(hidden.astype(jnp.bfloat16), dy)

    return step
```

profile of v0, /device:TPU:0, one launch (start us, length us, event | category | flops | bytes accessed | tf_op | source)
XLA Modules:
  0.0 1765.8 jit_solution(16699633523575936599)
XLA Ops:
  8.7 145.9 %all-gather.7.cloned.1.call-done = bf16[2560,7168]{1,0:T(8,128)(2,1)} async-done(((bf16[160,7168]{1,0:T(8,128)(2,1)}), bf16[2560,7168]{1,0:T(8,128)(2,1)}) %all-gather.7.cloned.1.call-update) | async-done | bytes 36700176 | tf_op args[1]
  154.6 72.2 %fusion.40 = (bf16[2560,1152]{1,0:T(8,128)(2,1)}, bf16[2560,1152]{1,0:T(8,128)(2,1)}) fusion(bf16[2560,1152]{1,0:T(8,128)(2,1)} %param.7, bf16[2560,1152]{1,0:T(8,128)(2,1)} %param.6, bf16[2560,7168]{1,0:T(8,128)(2,1)} %all-gather.7.cloned.1.call-done, bf16[1152,7168]{1,0:T(8,128)(2,1)} %param.5), kind=kOutput, calls=%fused_computation.65 | convolution fusion | flops 42325770240 | bytes 76808192 | tf_op jit(solution)/dot_general | solution.py:12
  226.8 659.0 %while.5 = (bf16[2560,1152]{1,0:T(8,128)(2,1)}, bf16[7168,1152]{1,0:T(8,128)(2,1)}, bf16[160,7168]{1,0:T(8,128)(2,1)}, bf16[160,7168]{1,0:T(8,128)(2,1)}, u32[]{...) while((bf16[2560,1152]{1,0:T(8,128)(2,1)}, ...), condition=%wide.windowed_dot_general_cond_rs.1.clone, body=%wide.windowed_dot_general_body_rs.1.clone.sunk | while | flops 10579476480 | bytes 136577664 | solution.py:14
  232.2 9.8 fusion.81
  242.0 63.4 %collective-permute-done.5 = bf16[160,7168]{1,0:T(8,128)(2,1)} collective-permute-done((bf16[160,7168]{1,0:T(8,128)(2,1)}, bf16[160,7168]{1,0:T(8,128)(2,1)}, u32[]{:S(2)}, u32[]{:S(2)}) %collective-permute-start.5) | collective-permute-done | bytes 2293792 | tf_op jit(solution)/dot_general | solution.py:14
  315.6 44.6 %collective-permute-start.6 = (bf16[160,7168]{1,0:T(8,128)(2,1)}, bf16[160,7168]{1,0:T(8,128)(2,1)}, u32[]{:S(2)}, u32[]{:S(2)}) collective-permute-start(bf16[160,7168]{1,0:T(8,128)(2,1)} %get-tuple-element.160), channel_id=12, source_target_pairs={{0,1},{1,2},{2,3},{3,4},{4,5},{5,6},{6,7},{7,8},{8,9},{9,10},{10,1... | collective-permute-start | bytes 6881288 | tf_op jit(solution)/dot_general | solution.py:14
  360.3 9.8 fusion.83
  370.1 15.9 collective-permute-done.7
  399.6 44.8 %collective-permute-start.4 = (bf16[160,7168]{1,0:T(8,128)(2,1)}, bf16[160,7168]{1,0:T(8,128)(2,1)}, u32[]{:S(2)}, u32[]{:S(2)}) collective-permute-start(bf16[160,7168]{1,0:T(8,128)(2,1)} %broadcast_select_fusion.10), channel_id=10, source_target_pairs={{0,1},{1,2},{2,3},{3,4},{4,5},{5,6},{6,7},{7,8},{8,9},{9,10},{10,1... | collective-permute-start | bytes 6881288 | tf_op jit(solution)/dot_general | solution.py:14
  454.1 20.3 %collective-permute-done.4 = bf16[160,7168]{1,0:T(8,128)(2,1)} collective-permute-done((bf16[160,7168]{1,0:T(8,128)(2,1)}, bf16[160,7168]{1,0:T(8,128)(2,1)}, u32[]{:S(2)}, u32[]{:S(2)}) %collective-permute-start.4) | collective-permute-done | bytes 2293792 | tf_op jit(solution)/dot_general | solution.py:14
  479.4 45.8 %collective-permute-start.6 = (bf16[160,7168]{1,0:T(8,128)(2,1)}, bf16[160,7168]{1,0:T(8,128)(2,1)}, u32[]{:S(2)}, u32[]{:S(2)}) collective-permute-start(bf16[160,7168]{1,0:T(8,128)(2,1)} %get-tuple-element.160), channel_id=12, source_target_pairs={{0,1},{1,2},{2,3},{3,4},{4,5},{5,6},{6,7},{7,8},{8,9},{9,10},{10,1... | collective-permute-start | bytes 6881288 | tf_op jit(solution)/dot_general | solution.py:14
  525.2 9.8 fusion.83
  535.1 15.9 collective-permute-done.7
  564.5 44.8 %collective-permute-start.4 = (bf16[160,7168]{1,0:T(8,128)(2,1)}, bf16[160,7168]{1,0:T(8,128)(2,1)}, u32[]{:S(2)}, u32[]{:S(2)}) collective-permute-start(bf16[160,7168]{1,0:T(8,128)(2,1)} %broadcast_select_fusion.10), channel_id=10, source_target_pairs={{0,1},{1,2},{2,3},{3,4},{4,5},{5,6},{6,7},{7,8},{8,9},{9,10},{10,1... | collective-permute-start | bytes 6881288 | tf_op jit(solution)/dot_general | solution.py:14
  619.1 20.3 %collective-permute-done.4 = bf16[160,7168]{1,0:T(8,128)(2,1)} collective-permute-done((bf16[160,7168]{1,0:T(8,128)(2,1)}, bf16[160,7168]{1,0:T(8,128)(2,1)}, u32[]{:S(2)}, u32[]{:S(2)}) %collective-permute-start.4) | collective-permute-done | bytes 2293792 | tf_op jit(solution)/dot_general | solution.py:14
  644.4 45.8 %collective-permute-start.6 = (bf16[160,7168]{1,0:T(8,128)(2,1)}, bf16[160,7168]{1,0:T(8,128)(2,1)}, u32[]{:S(2)}, u32[]{:S(2)}) collective-permute-start(bf16[160,7168]{1,0:T(8,128)(2,1)} %get-tuple-element.160), channel_id=12, source_target_pairs={{0,1},{1,2},{2,3},{3,4},{4,5},{5,6},{6,7},{7,8},{8,9},{9,10},{10,1... | collective-permute-start | bytes 6881288 | tf_op jit(solution)/dot_general | solution.py:14
  690.2 9.8 fusion.83
  700.0 15.9 collective-permute-done.7
  729.5 44.8 %collective-permute-start.4 = (bf16[160,7168]{1,0:T(8,128)(2,1)}, bf16[160,7168]{1,0:T(8,128)(2,1)}, u32[]{:S(2)}, u32[]{:S(2)}) collective-permute-start(bf16[160,7168]{1,0:T(8,128)(2,1)} %broadcast_select_fusion.10), channel_id=10, source_target_pairs={{0,1},{1,2},{2,3},{3,4},{4,5},{5,6},{6,7},{7,8},{8,9},{9,10},{10,1... | collective-permute-start | bytes 6881288 | tf_op jit(solution)/dot_general | solution.py:14
  784.1 20.3 %collective-permute-done.4 = bf16[160,7168]{1,0:T(8,128)(2,1)} collective-permute-done((bf16[160,7168]{1,0:T(8,128)(2,1)}, bf16[160,7168]{1,0:T(8,128)(2,1)}, u32[]{:S(2)}, u32[]{:S(2)}) %collective-permute-start.4) | collective-permute-done | bytes 2293792 | tf_op jit(solution)/dot_general | solution.py:14
  809.3 45.8 %collective-permute-start.6 = (bf16[160,7168]{1,0:T(8,128)(2,1)}, bf16[160,7168]{1,0:T(8,128)(2,1)}, u32[]{:S(2)}, u32[]{:S(2)}) collective-permute-start(bf16[160,7168]{1,0:T(8,128)(2,1)} %get-tuple-element.160), channel_id=12, source_target_pairs={{0,1},{1,2},{2,3},{3,4},{4,5},{5,6},{6,7},{7,8},{8,9},{9,10},{10,1... | collective-permute-start | bytes 6881288 | tf_op jit(solution)/dot_general | solution.py:14
  855.2 9.8 fusion.83
  865.0 15.9 collective-permute-done.7
  885.8 23.9 %collective-permute-start.9 = (bf16[160,7168]{1,0:T(8,128)(2,1)}, bf16[160,7168]{1,0:T(8,128)(2,1)}, u32[]{:S(2)}, u32[]{:S(2)}) collective-permute-start(bf16[160,7168]{1,0:T(8,128)(2,1)} %get-tuple-element.15), channel_id=13, source_target_pairs={{0,1},{1,2},{2,3},{3,4},{4,5},{5,6},{6,7},{7,8},{8,9},{9,10},{10,1... | collective-permute-start | bytes 6881288 | tf_op jit(solution)/dot_general | solution.py:14
  909.7 615.6 %while.4 = (bf16[2560,1152]{1,0:T(8,128)(2,1)}, bf16[7168,1152]{1,0:T(8,128)(2,1)}, bf16[160,7168]{1,0:T(8,128)(2,1)S(1)}, bf16[160,7168]{1,0:T(8,128)(2,1)}, u3...) while((bf16[2560,1152]{1,0:T(8,128)(2,1)}, ...), condition=%wide.windowed_dot_general_cond_rs.clone, body=%wide.windowed_dot_general_body_rs.clone.sunk | while | flops 10579476480 | bytes 145752736 | solution.py:14
  935.3 11.1 collective-permute-done.1
  956.7 48.9 %collective-permute-start.2 = (bf16[160,7168]{1,0:T(8,128)(2,1)}, bf16[160,7168]{1,0:T(8,128)(2,1)}, u32[]{:S(2)}, u32[]{:S(2)}) collective-permute-start(bf16[160,7168]{1,0:T(8,128)(2,1)} %get-tuple-element.151), channel_id=6, source_target_pairs={{0,1},{1,2},{2,3},{3,4},{4,5},{5,6},{6,7},{7,8},{8,9},{9,10},{10,1... | collective-permute-start | bytes 6881288 | tf_op jit(solution)/dot_general | solution.py:14
  1005.6 9.8 fusion.75
  1015.4 15.9 collective-permute-done.3
  1042.5 45.5 %collective-permute-start = (bf16[160,7168]{1,0:T(8,128)(2,1)}, bf16[160,7168]{1,0:T(8,128)(2,1)}, u32[]{:S(2)}, u32[]{:S(2)}) collective-permute-start(bf16[160,7168]{1,0:T(8,128)(2,1)} %broadcast_select_fusion.8), channel_id=4, source_target_pairs={{0,1},{1,2},{2,3},{3,4},{4,5},{5,6},{6,7},{7,8},{8,9},{9,10},{10,1... | collective-permute-start | bytes 6881288 | tf_op jit(solution)/dot_general | solution.py:14
  1099.4 18.0 %collective-permute-done = bf16[160,7168]{1,0:T(8,128)(2,1)} collective-permute-done((bf16[160,7168]{1,0:T(8,128)(2,1)}, bf16[160,7168]{1,0:T(8,128)(2,1)}, u32[]{:S(2)}, u32[]{:S(2)}) %collective-permute-start) | collective-permute-done | bytes 2293792 | tf_op jit(solution)/dot_general | solution.py:14
  1121.5 47.4 %collective-permute-start.2 = (bf16[160,7168]{1,0:T(8,128)(2,1)}, bf16[160,7168]{1,0:T(8,128)(2,1)}, u32[]{:S(2)}, u32[]{:S(2)}) collective-permute-start(bf16[160,7168]{1,0:T(8,128)(2,1)} %get-tuple-element.151), channel_id=6, source_target_pairs={{0,1},{1,2},{2,3},{3,4},{4,5},{5,6},{6,7},{7,8},{8,9},{9,10},{10,1... | collective-permute-start | bytes 6881288 | tf_op jit(solution)/dot_general | solution.py:14
  1178.7 15.9 collective-permute-done.3
  1205.8 45.5 %collective-permute-start = (bf16[160,7168]{1,0:T(8,128)(2,1)}, bf16[160,7168]{1,0:T(8,128)(2,1)}, u32[]{:S(2)}, u32[]{:S(2)}) collective-permute-start(bf16[160,7168]{1,0:T(8,128)(2,1)} %broadcast_select_fusion.8), channel_id=4, source_target_pairs={{0,1},{1,2},{2,3},{3,4},{4,5},{5,6},{6,7},{7,8},{8,9},{9,10},{10,1... | collective-permute-start | bytes 6881288 | tf_op jit(solution)/dot_general | solution.py:14
  1251.3 9.8 fusion.73
  1262.7 18.0 %collective-permute-done = bf16[160,7168]{1,0:T(8,128)(2,1)} collective-permute-done((bf16[160,7168]{1,0:T(8,128)(2,1)}, bf16[160,7168]{1,0:T(8,128)(2,1)}, u32[]{:S(2)}, u32[]{:S(2)}) %collective-permute-start) | collective-permute-done | bytes 2293792 | tf_op jit(solution)/dot_general | solution.py:14
  1284.8 47.4 %collective-permute-start.2 = (bf16[160,7168]{1,0:T(8,128)(2,1)}, bf16[160,7168]{1,0:T(8,128)(2,1)}, u32[]{:S(2)}, u32[]{:S(2)}) collective-permute-start(bf16[160,7168]{1,0:T(8,128)(2,1)} %get-tuple-element.151), channel_id=6, source_target_pairs={{0,1},{1,2},{2,3},{3,4},{4,5},{5,6},{6,7},{7,8},{8,9},{9,10},{10,1... | collective-permute-start | bytes 6881288 | tf_op jit(solution)/dot_general | solution.py:14
  1342.0 15.9 collective-permute-done.3
  1369.1 45.5 %collective-permute-start = (bf16[160,7168]{1,0:T(8,128)(2,1)}, bf16[160,7168]{1,0:T(8,128)(2,1)}, u32[]{:S(2)}, u32[]{:S(2)}) collective-permute-start(bf16[160,7168]{1,0:T(8,128)(2,1)} %broadcast_select_fusion.8), channel_id=4, source_target_pairs={{0,1},{1,2},{2,3},{3,4},{4,5},{5,6},{6,7},{7,8},{8,9},{9,10},{10,1... | collective-permute-start | bytes 6881288 | tf_op jit(solution)/dot_general | solution.py:14
  1426.0 18.0 %collective-permute-done = bf16[160,7168]{1,0:T(8,128)(2,1)} collective-permute-done((bf16[160,7168]{1,0:T(8,128)(2,1)}, bf16[160,7168]{1,0:T(8,128)(2,1)}, u32[]{:S(2)}, u32[]{:S(2)}) %collective-permute-start) | collective-permute-done | bytes 2293792 | tf_op jit(solution)/dot_general | solution.py:14
  1448.1 47.4 %collective-permute-start.2 = (bf16[160,7168]{1,0:T(8,128)(2,1)}, bf16[160,7168]{1,0:T(8,128)(2,1)}, u32[]{:S(2)}, u32[]{:S(2)}) collective-permute-start(bf16[160,7168]{1,0:T(8,128)(2,1)} %get-tuple-element.151), channel_id=6, source_target_pairs={{0,1},{1,2},{2,3},{3,4},{4,5},{5,6},{6,7},{7,8},{8,9},{9,10},{10,1... | collective-permute-start | bytes 6881288 | tf_op jit(solution)/dot_general | solution.py:14
  1505.3 15.9 collective-permute-done.3
  1525.4 23.9 %collective-permute-start.8 = (bf16[160,7168]{1,0:T(8,128)(2,1)}, bf16[160,7168]{1,0:T(8,128)(2,1)}, u32[]{:S(2)}, u32[]{:S(2)}) collective-permute-start(bf16[160,7168]{1,0:T(8,128)(2,1)} %get-tuple-element.13), channel_id=7, source_target_pairs={{0,1},{1,2},{2,3},{3,4},{4,5},{5,6},{6,7},{7,8},{8,9},{9,10},{10,1... | collective-permute-start | bytes 6881288 | tf_op jit(solution)/dot_general | solution.py:14
  1549.3 61.1 %convolution_convert_fusion = bf16[1152,7168]{1,0:T(8,128)(2,1)} fusion(bf16[2560,7168]{1,0:T(8,128)(2,1)} %all-gather.7.cloned.1.call-done, bf16[2560,1152]{1,0:T(8,128)(2,1)} %param.6, bf16[2560,1152]{1,0:T(8,128)(2,1)} %param.7), kind=kOutput, calls=%fused_computation.48 | convolution fusion | flops 42310434816 | bytes 65011712 | tf_op jit(solution)/gta,gtb->gab/dot_general | solution.py:19
  1610.4 50.4 %fusion.32 = bf16[7168,1152]{0,1:T(8,128)(2,1)} fusion(bf16[2560,1152]{1,0:T(8,128)(2,1)} %get-tuple-element.249, bf16[2560,7168]{1,0:T(8,128)(2,1)} %all-gather.9.cloned.1.call-done), kind=kOutput, calls=%fused_computation.51 | convolution fusion | flops 42286841856 | bytes 59113472 | tf_op jit(solution)/gta,gtb->gab/dot_general | solution.py:19
  1660.8 48.2 %fusion.33 = bf16[7168,1152]{0,1:T(8,128)(2,1)} fusion(bf16[2560,1152]{1,0:T(8,128)(2,1)S(1)} %copy-done.6, bf16[2560,7168]{1,0:T(8,128)(2,1)} %all-gather.9.cloned.1.call-done), kind=kOutput, calls=%fused_computation.52 | convolution fusion | flops 42286841856 | bytes 59113472 | tf_op jit(solution)/gta,gtb->gab/dot_general | solution.py:19
  1709.1 22.2 %copy.1 = bf16[7168,1152]{1,0:T(8,128)(2,1)} copy(bf16[7168,1152]{0,1:T(8,128)(2,1)} %fusion.33) | data formatting | bytes 33030144
  1731.3 22.4 %copy = bf16[7168,1152]{1,0:T(8,128)(2,1)} copy(bf16[7168,1152]{0,1:T(8,128)(2,1)} %fusion.32) | data formatting | bytes 33030144
  (119 shorter events, 242.2 us)
Async XLA Ops:
  7.2 147.5 %all-gather.7.cloned.1.call-start = ((), (), s32[]{:S(2)}) async-start(), calls=%async_computation | async-start | bytes 38993920 | tf_op args[1]
  7.9 1602.5 %all-gather.9.cloned.1.call-start = ((), (), s32[]{:S(2)}) async-start(), calls=%async_computation.1 | async-start | bytes 38993920 | tf_op args[0]
  226.8 682.9 %copy-start = (bf16[160,7168]{1,0:T(8,128)(2,1)S(1)}, bf16[160,7168]{1,0:T(8,128)(2,1)}, u32[]{:S(2)}) copy-start(bf16[160,7168]{1,0:T(8,128)(2,1)} %custom-call) | copy-start | bytes 6881284
  226.8 3.8 copy-start.5
  228.4 77.0 %collective-permute-start.5 = (bf16[160,7168]{1,0:T(8,128)(2,1)}, bf16[160,7168]{1,0:T(8,128)(2,1)}, u32[]{:S(2)}, u32[]{:S(2)}) collective-permute-start(bf16[160,7168]{1,0:T(8,128)(2,1)} %broadcast_select_fusion.11), channel_id=9, source_target_pairs={{0,15},{1,0},{2,1},{3,2},{4,3},{5,4},{6,5},{7,6},{8,7},{9,8},{10,9... | collective-permute-start | bytes 6881288 | tf_op jit(solution)/dot_general | solution.py:14
  232.2 78.5 %collective-permute-start.4 = (bf16[160,7168]{1,0:T(8,128)(2,1)}, bf16[160,7168]{1,0:T(8,128)(2,1)}, u32[]{:S(2)}, u32[]{:S(2)}) collective-permute-start(bf16[160,7168]{1,0:T(8,128)(2,1)} %broadcast_select_fusion.10), channel_id=10, source_target_pairs={{0,1},{1,2},{2,3},{3,4},{4,5},{5,6},{6,7},{7,8},{8,9},{9,10},{10,1... | collective-permute-start | bytes 6881288 | tf_op jit(solution)/dot_general | solution.py:14
  315.6 54.4 %collective-permute-start.6 = (bf16[160,7168]{1,0:T(8,128)(2,1)}, bf16[160,7168]{1,0:T(8,128)(2,1)}, u32[]{:S(2)}, u32[]{:S(2)}) collective-permute-start(bf16[160,7168]{1,0:T(8,128)(2,1)} %get-tuple-element.160), channel_id=12, source_target_pairs={{0,1},{1,2},{2,3},{3,4},{4,5},{5,6},{6,7},{7,8},{8,9},{9,10},{10,1... | collective-permute-start | bytes 6881288 | tf_op jit(solution)/dot_general | solution.py:14
  360.3 25.7 %collective-permute-start.7 = (bf16[160,7168]{1,0:T(8,128)(2,1)}, bf16[160,7168]{1,0:T(8,128)(2,1)}, u32[]{:S(2)}, u32[]{:S(2)}) collective-permute-start(bf16[160,7168]{1,0:T(8,128)(2,1)} %get-tuple-element.161), channel_id=11, source_target_pairs={{0,15},{1,0},{2,1},{3,2},{4,3},{5,4},{6,5},{7,6},{8,7},{9,8},{10,9... | collective-permute-start | bytes 6881288 | tf_op jit(solution)/dot_general | solution.py:14
  390.9 7.1 copy-start.5
  394.3 59.8 %collective-permute-start.5 = (bf16[160,7168]{1,0:T(8,128)(2,1)}, bf16[160,7168]{1,0:T(8,128)(2,1)}, u32[]{:S(2)}, u32[]{:S(2)}) collective-permute-start(bf16[160,7168]{1,0:T(8,128)(2,1)} %broadcast_select_fusion.11), channel_id=9, source_target_pairs={{0,15},{1,0},{2,1},{3,2},{4,3},{5,4},{6,5},{7,6},{8,7},{9,8},{10,9... | collective-permute-start | bytes 6881288 | tf_op jit(solution)/dot_general | solution.py:14
  399.6 74.9 %collective-permute-start.4 = (bf16[160,7168]{1,0:T(8,128)(2,1)}, bf16[160,7168]{1,0:T(8,128)(2,1)}, u32[]{:S(2)}, u32[]{:S(2)}) collective-permute-start(bf16[160,7168]{1,0:T(8,128)(2,1)} %broadcast_select_fusion.10), channel_id=10, source_target_pairs={{0,1},{1,2},{2,3},{3,4},{4,5},{5,6},{6,7},{7,8},{8,9},{9,10},{10,1... | collective-permute-start | bytes 6881288 | tf_op jit(solution)/dot_general | solution.py:14
  479.4 55.6 %collective-permute-start.6 = (bf16[160,7168]{1,0:T(8,128)(2,1)}, bf16[160,7168]{1,0:T(8,128)(2,1)}, u32[]{:S(2)}, u32[]{:S(2)}) collective-permute-start(bf16[160,7168]{1,0:T(8,128)(2,1)} %get-tuple-element.160), channel_id=12, source_target_pairs={{0,1},{1,2},{2,3},{3,4},{4,5},{5,6},{6,7},{7,8},{8,9},{9,10},{10,1... | collective-permute-start | bytes 6881288 | tf_op jit(solution)/dot_general | solution.py:14
  525.2 25.7 %collective-permute-start.7 = (bf16[160,7168]{1,0:T(8,128)(2,1)}, bf16[160,7168]{1,0:T(8,128)(2,1)}, u32[]{:S(2)}, u32[]{:S(2)}) collective-permute-start(bf16[160,7168]{1,0:T(8,128)(2,1)} %get-tuple-element.161), channel_id=11, source_target_pairs={{0,15},{1,0},{2,1},{3,2},{4,3},{5,4},{6,5},{7,6},{8,7},{9,8},{10,9... | collective-permute-start | bytes 6881288 | tf_op jit(solution)/dot_general | solution.py:14
  555.9 7.1 copy-start.5
  559.3 59.8 %collective-permute-start.5 = (bf16[160,7168]{1,0:T(8,128)(2,1)}, bf16[160,7168]{1,0:T(8,128)(2,1)}, u32[]{:S(2)}, u32[]{:S(2)}) collective-permute-start(bf16[160,7168]{1,0:T(8,128)(2,1)} %broadcast_select_fusion.11), channel_id=9, source_target_pairs={{0,15},{1,0},{2,1},{3,2},{4,3},{5,4},{6,5},{7,6},{8,7},{9,8},{10,9... | collective-permute-start | bytes 6881288 | tf_op jit(solution)/dot_general | solution.py:14
  564.5 74.9 %collective-permute-start.4 = (bf16[160,7168]{1,0:T(8,128)(2,1)}, bf16[160,7168]{1,0:T(8,128)(2,1)}, u32[]{:S(2)}, u32[]{:S(2)}) collective-permute-start(bf16[160,7168]{1,0:T(8,128)(2,1)} %broadcast_select_fusion.10), channel_id=10, source_target_pairs={{0,1},{1,2},{2,3},{3,4},{4,5},{5,6},{6,7},{7,8},{8,9},{9,10},{10,1... | collective-permute-start | bytes 6881288 | tf_op jit(solution)/dot_general | solution.py:14
  644.4 55.6 %collective-permute-start.6 = (bf16[160,7168]{1,0:T(8,128)(2,1)}, bf16[160,7168]{1,0:T(8,128)(2,1)}, u32[]{:S(2)}, u32[]{:S(2)}) collective-permute-start(bf16[160,7168]{1,0:T(8,128)(2,1)} %get-tuple-element.160), channel_id=12, source_target_pairs={{0,1},{1,2},{2,3},{3,4},{4,5},{5,6},{6,7},{7,8},{8,9},{9,10},{10,1... | collective-permute-start | bytes 6881288 | tf_op jit(solution)/dot_general | solution.py:14
  690.2 25.7 %collective-permute-start.7 = (bf16[160,7168]{1,0:T(8,128)(2,1)}, bf16[160,7168]{1,0:T(8,128)(2,1)}, u32[]{:S(2)}, u32[]{:S(2)}) collective-permute-start(bf16[160,7168]{1,0:T(8,128)(2,1)} %get-tuple-element.161), channel_id=11, source_target_pairs={{0,15},{1,0},{2,1},{3,2},{4,3},{5,4},{6,5},{7,6},{8,7},{9,8},{10,9... | collective-permute-start | bytes 6881288 | tf_op jit(solution)/dot_general | solution.py:14
  720.9 7.1 copy-start.5
  724.2 59.8 %collective-permute-start.5 = (bf16[160,7168]{1,0:T(8,128)(2,1)}, bf16[160,7168]{1,0:T(8,128)(2,1)}, u32[]{:S(2)}, u32[]{:S(2)}) collective-permute-start(bf16[160,7168]{1,0:T(8,128)(2,1)} %broadcast_select_fusion.11), channel_id=9, source_target_pairs={{0,15},{1,0},{2,1},{3,2},{4,3},{5,4},{6,5},{7,6},{8,7},{9,8},{10,9... | collective-permute-start | bytes 6881288 | tf_op jit(solution)/dot_general | solution.py:14
  729.5 74.9 %collective-permute-start.4 = (bf16[160,7168]{1,0:T(8,128)(2,1)}, bf16[160,7168]{1,0:T(8,128)(2,1)}, u32[]{:S(2)}, u32[]{:S(2)}) collective-permute-start(bf16[160,7168]{1,0:T(8,128)(2,1)} %broadcast_select_fusion.10), channel_id=10, source_target_pairs={{0,1},{1,2},{2,3},{3,4},{4,5},{5,6},{6,7},{7,8},{8,9},{9,10},{10,1... | collective-permute-start | bytes 6881288 | tf_op jit(solution)/dot_general | solution.py:14
  809.3 55.6 %collective-permute-start.6 = (bf16[160,7168]{1,0:T(8,128)(2,1)}, bf16[160,7168]{1,0:T(8,128)(2,1)}, u32[]{:S(2)}, u32[]{:S(2)}) collective-permute-start(bf16[160,7168]{1,0:T(8,128)(2,1)} %get-tuple-element.160), channel_id=12, source_target_pairs={{0,1},{1,2},{2,3},{3,4},{4,5},{5,6},{6,7},{7,8},{8,9},{9,10},{10,1... | collective-permute-start | bytes 6881288 | tf_op jit(solution)/dot_general | solution.py:14
  855.2 25.7 %collective-permute-start.7 = (bf16[160,7168]{1,0:T(8,128)(2,1)}, bf16[160,7168]{1,0:T(8,128)(2,1)}, u32[]{:S(2)}, u32[]{:S(2)}) collective-permute-start(bf16[160,7168]{1,0:T(8,128)(2,1)} %get-tuple-element.161), channel_id=11, source_target_pairs={{0,15},{1,0},{2,1},{3,2},{4,3},{5,4},{6,5},{7,6},{8,7},{9,8},{10,9... | collective-permute-start | bytes 6881288 | tf_op jit(solution)/dot_general | solution.py:14
  885.8 867.9 %collective-permute-start.9 = (bf16[160,7168]{1,0:T(8,128)(2,1)}, bf16[160,7168]{1,0:T(8,128)(2,1)}, u32[]{:S(2)}, u32[]{:S(2)}) collective-permute-start(bf16[160,7168]{1,0:T(8,128)(2,1)} %get-tuple-element.15), channel_id=13, source_target_pairs={{0,1},{1,2},{2,3},{3,4},{4,5},{5,6},{6,7},{7,8},{8,9},{9,10},{10,1... | collective-permute-start | bytes 6881288 | tf_op jit(solution)/dot_general | solution.py:14
  918.9 2.5 copy-start.4
  920.7 25.7 %collective-permute-start.1 = (bf16[160,7168]{1,0:T(8,128)(2,1)}, bf16[160,7168]{1,0:T(8,128)(2,1)S(1)}, u32[]{:S(2)}, u32[]{:S(2)}) collective-permute-start(bf16[160,7168]{1,0:T(8,128)(2,1)} %broadcast_select_fusion.9), channel_id=3, source_target_pairs={{0,15},{1,0},{2,1},{3,2},{4,3},{5,4},{6,5},{7,6},{8,7},{9,8},{10,9... | collective-permute-start | bytes 6881288 | tf_op jit(solution)/dot_general | solution.py:14
  923.0 29.6 %collective-permute-start = (bf16[160,7168]{1,0:T(8,128)(2,1)}, bf16[160,7168]{1,0:T(8,128)(2,1)}, u32[]{:S(2)}, u32[]{:S(2)}) collective-permute-start(bf16[160,7168]{1,0:T(8,128)(2,1)} %broadcast_select_fusion.8), channel_id=4, source_target_pairs={{0,1},{1,2},{2,3},{3,4},{4,5},{5,6},{6,7},{7,8},{8,9},{9,10},{10,1... | collective-permute-start | bytes 6881288 | tf_op jit(solution)/dot_general | solution.py:14
  956.7 58.7 %collective-permute-start.2 = (bf16[160,7168]{1,0:T(8,128)(2,1)}, bf16[160,7168]{1,0:T(8,128)(2,1)}, u32[]{:S(2)}, u32[]{:S(2)}) collective-permute-start(bf16[160,7168]{1,0:T(8,128)(2,1)} %get-tuple-element.151), channel_id=6, source_target_pairs={{0,1},{1,2},{2,3},{3,4},{4,5},{5,6},{6,7},{7,8},{8,9},{9,10},{10,1... | collective-permute-start | bytes 6881288 | tf_op jit(solution)/dot_general | solution.py:14
  1005.6 25.7 %collective-permute-start.3 = (bf16[160,7168]{1,0:T(8,128)(2,1)S(1)}, bf16[160,7168]{1,0:T(8,128)(2,1)}, u32[]{:S(2)}, u32[]{:S(2)}) collective-permute-start(bf16[160,7168]{1,0:T(8,128)(2,1)S(1)} %get-tuple-element.152), channel_id=5, source_target_pairs={{0,15},{1,0},{2,1},{3,2},{4,3},{5,4},{6,5},{7,6},{8,7},{9,8},{10,9... | collective-permute-start | bytes 6881288 | tf_op jit(solution)/dot_general | solution.py:14
  1035.5 5.4 copy-start.4
  1037.2 60.6 %collective-permute-start.1 = (bf16[160,7168]{1,0:T(8,128)(2,1)}, bf16[160,7168]{1,0:T(8,128)(2,1)S(1)}, u32[]{:S(2)}, u32[]{:S(2)}) collective-permute-start(bf16[160,7168]{1,0:T(8,128)(2,1)} %broadcast_select_fusion.9), channel_id=3, source_target_pairs={{0,15},{1,0},{2,1},{3,2},{4,3},{5,4},{6,5},{7,6},{8,7},{9,8},{10,9... | collective-permute-start | bytes 6881288 | tf_op jit(solution)/dot_general | solution.py:14
  1042.5 74.9 %collective-permute-start = (bf16[160,7168]{1,0:T(8,128)(2,1)}, bf16[160,7168]{1,0:T(8,128)(2,1)}, u32[]{:S(2)}, u32[]{:S(2)}) collective-permute-start(bf16[160,7168]{1,0:T(8,128)(2,1)} %broadcast_select_fusion.8), channel_id=4, source_target_pairs={{0,1},{1,2},{2,3},{3,4},{4,5},{5,6},{6,7},{7,8},{8,9},{9,10},{10,1... | collective-permute-start | bytes 6881288 | tf_op jit(solution)/dot_general | solution.py:14
  1121.5 57.2 %collective-permute-start.2 = (bf16[160,7168]{1,0:T(8,128)(2,1)}, bf16[160,7168]{1,0:T(8,128)(2,1)}, u32[]{:S(2)}, u32[]{:S(2)}) collective-permute-start(bf16[160,7168]{1,0:T(8,128)(2,1)} %get-tuple-element.151), channel_id=6, source_target_pairs={{0,1},{1,2},{2,3},{3,4},{4,5},{5,6},{6,7},{7,8},{8,9},{9,10},{10,1... | collective-permute-start | bytes 6881288 | tf_op jit(solution)/dot_general | solution.py:14
  1168.9 25.7 %collective-permute-start.3 = (bf16[160,7168]{1,0:T(8,128)(2,1)S(1)}, bf16[160,7168]{1,0:T(8,128)(2,1)}, u32[]{:S(2)}, u32[]{:S(2)}) collective-permute-start(bf16[160,7168]{1,0:T(8,128)(2,1)S(1)} %get-tuple-element.152), channel_id=5, source_target_pairs={{0,15},{1,0},{2,1},{3,2},{4,3},{5,4},{6,5},{7,6},{8,7},{9,8},{10,9... | collective-permute-start | bytes 6881288 | tf_op jit(solution)/dot_general | solution.py:14
  1198.8 5.4 copy-start.4
  1200.5 60.6 %collective-permute-start.1 = (bf16[160,7168]{1,0:T(8,128)(2,1)}, bf16[160,7168]{1,0:T(8,128)(2,1)S(1)}, u32[]{:S(2)}, u32[]{:S(2)}) collective-permute-start(bf16[160,7168]{1,0:T(8,128)(2,1)} %broadcast_select_fusion.9), channel_id=3, source_target_pairs={{0,15},{1,0},{2,1},{3,2},{4,3},{5,4},{6,5},{7,6},{8,7},{9,8},{10,9... | collective-permute-start | bytes 6881288 | tf_op jit(solution)/dot_general | solution.py:14
  1205.8 74.9 %collective-permute-start = (bf16[160,7168]{1,0:T(8,128)(2,1)}, bf16[160,7168]{1,0:T(8,128)(2,1)}, u32[]{:S(2)}, u32[]{:S(2)}) collective-permute-start(bf16[160,7168]{1,0:T(8,128)(2,1)} %broadcast_select_fusion.8), channel_id=4, source_target_pairs={{0,1},{1,2},{2,3},{3,4},{4,5},{5,6},{6,7},{7,8},{8,9},{9,10},{10,1... | collective-permute-start | bytes 6881288 | tf_op jit(solution)/dot_general | solution.py:14
  1284.8 57.2 %collective-permute-start.2 = (bf16[160,7168]{1,0:T(8,128)(2,1)}, bf16[160,7168]{1,0:T(8,128)(2,1)}, u32[]{:S(2)}, u32[]{:S(2)}) collective-permute-start(bf16[160,7168]{1,0:T(8,128)(2,1)} %get-tuple-element.151), channel_id=6, source_target_pairs={{0,1},{1,2},{2,3},{3,4},{4,5},{5,6},{6,7},{7,8},{8,9},{9,10},{10,1... | collective-permute-start | bytes 6881288 | tf_op jit(solution)/dot_general | solution.py:14
  1332.2 25.7 %collective-permute-start.3 = (bf16[160,7168]{1,0:T(8,128)(2,1)S(1)}, bf16[160,7168]{1,0:T(8,128)(2,1)}, u32[]{:S(2)}, u32[]{:S(2)}) collective-permute-start(bf16[160,7168]{1,0:T(8,128)(2,1)S(1)} %get-tuple-element.152), channel_id=5, source_target_pairs={{0,15},{1,0},{2,1},{3,2},{4,3},{5,4},{6,5},{7,6},{8,7},{9,8},{10,9... | collective-permute-start | bytes 6881288 | tf_op jit(solution)/dot_general | solution.py:14
  1362.1 5.4 copy-start.4
  1363.8 60.6 %collective-permute-start.1 = (bf16[160,7168]{1,0:T(8,128)(2,1)}, bf16[160,7168]{1,0:T(8,128)(2,1)S(1)}, u32[]{:S(2)}, u32[]{:S(2)}) collective-permute-start(bf16[160,7168]{1,0:T(8,128)(2,1)} %broadcast_select_fusion.9), channel_id=3, source_target_pairs={{0,15},{1,0},{2,1},{3,2},{4,3},{5,4},{6,5},{7,6},{8,7},{9,8},{10,9... | collective-permute-start | bytes 6881288 | tf_op jit(solution)/dot_general | solution.py:14
  1369.1 74.9 %collective-permute-start = (bf16[160,7168]{1,0:T(8,128)(2,1)}, bf16[160,7168]{1,0:T(8,128)(2,1)}, u32[]{:S(2)}, u32[]{:S(2)}) collective-permute-start(bf16[160,7168]{1,0:T(8,128)(2,1)} %broadcast_select_fusion.8), channel_id=4, source_target_pairs={{0,1},{1,2},{2,3},{3,4},{4,5},{5,6},{6,7},{7,8},{8,9},{9,10},{10,1... | collective-permute-start | bytes 6881288 | tf_op jit(solution)/dot_general | solution.py:14
  1448.1 57.2 %collective-permute-start.2 = (bf16[160,7168]{1,0:T(8,128)(2,1)}, bf16[160,7168]{1,0:T(8,128)(2,1)}, u32[]{:S(2)}, u32[]{:S(2)}) collective-permute-start(bf16[160,7168]{1,0:T(8,128)(2,1)} %get-tuple-element.151), channel_id=6, source_target_pairs={{0,1},{1,2},{2,3},{3,4},{4,5},{5,6},{6,7},{7,8},{8,9},{9,10},{10,1... | collective-permute-start | bytes 6881288 | tf_op jit(solution)/dot_general | solution.py:14
  1495.5 25.7 %collective-permute-start.3 = (bf16[160,7168]{1,0:T(8,128)(2,1)S(1)}, bf16[160,7168]{1,0:T(8,128)(2,1)}, u32[]{:S(2)}, u32[]{:S(2)}) collective-permute-start(bf16[160,7168]{1,0:T(8,128)(2,1)S(1)} %get-tuple-element.152), channel_id=5, source_target_pairs={{0,15},{1,0},{2,1},{3,2},{4,3},{5,4},{6,5},{7,6},{8,7},{9,8},{10,9... | collective-permute-start | bytes 6881288 | tf_op jit(solution)/dot_general | solution.py:14
  1525.4 85.0 %copy-start.1 = (bf16[160,7168]{1,0:T(8,128)(2,1)}, bf16[160,7168]{1,0:T(8,128)(2,1)S(1)}, u32[]{:S(2)}) copy-start(bf16[160,7168]{1,0:T(8,128)(2,1)S(1)} %get-tuple-element.12) | copy-start | bytes 6881284
  1525.4 228.3 %collective-permute-start.8 = (bf16[160,7168]{1,0:T(8,128)(2,1)}, bf16[160,7168]{1,0:T(8,128)(2,1)}, u32[]{:S(2)}, u32[]{:S(2)}) collective-permute-start(bf16[160,7168]{1,0:T(8,128)(2,1)} %get-tuple-element.13), channel_id=7, source_target_pairs={{0,1},{1,2},{2,3},{3,4},{4,5},{5,6},{6,7},{7,8},{8,9},{9,10},{10,1... | collective-permute-start | bytes 6881288 | tf_op jit(solution)/dot_general | solution.py:14
  1610.4 50.4 %copy-start.6 = (bf16[2560,1152]{1,0:T(8,128)(2,1)S(1)}, bf16[2560,1152]{1,0:T(8,128)(2,1)}, u32[]{:S(2)}) copy-start(bf16[2560,1152]{1,0:T(8,128)(2,1)} %get-tuple-element.248) | copy-start | bytes 17694724
  1731.3 22.4 %copy-start.2 = (bf16[160,7168]{1,0:T(8,128)(2,1)S(1)}, bf16[160,7168]{1,0:T(8,128)(2,1)}, u32[]{:S(2)}) copy-start(bf16[160,7168]{1,0:T(8,128)(2,1)} %copy-done.1) | copy-start | bytes 6881284
  (4 other events, 6.2 us)
Sparse Core Ops, SparseCore 0:
  10.2 144.3 all-gather.6
  156.9 218.4 all-gather.8
where the time goes:
time: 1780 us; the launch traced here: 1770 us
  starting transfers between devices  719 us (40%)
  waiting for transfers between devices  474 us (27%)
  matrix products  389 us (22%)
  other arithmetic  109 us (6%)
  local copies, waits for them, and re-layouts  51.6 us (3%)
    dot_general x34, starting transfers between devices, step(): dx = jnp.dot(d_gate, w_gate.T) + jnp.dot(d_up, w_up.T)  719 us
    dot_general x34, waiting for transfers between devices, step(): dx = jnp.dot(d_gate, w_gate.T) + jnp.dot(d_up, w_up.T)  327 us
    dot_general x3, matrix products, by_group(): jnp.einsum('gta,gtb->gab', a, b, preferred_element_type=jnp.float32)  160 us
    dot_general x16, matrix products, step(): dx = jnp.dot(d_gate, w_gate.T) + jnp.dot(d_up, w_up.T)  157 us
    unnamed x4, waiting for transfers between devices  147 us
    dot_general x16, other arithmetic, step(): dx = jnp.dot(d_gate, w_gate.T) + jnp.dot(d_up, w_up.T)  72.9 us
    dot_general x1, matrix products, step(): d_hidden = jnp.dot(dy, w_down.T, preferred_element_type=jnp.float32)  72.2 us
    unnamed x10, local copies, waits for them, and re-layouts  44.6 us
  transfers between devices with their start and end apart: 36, of which 19 were waited for; matrix products, arithmetic and copies ran while one was open for 30% of the time, Pallas kernels for 0%

commit v1 on v0

v1 whole, which is shorter than its diff:
```python
import jax
import jax.numpy as jnp
from jax import lax
from jax.experimental import pallas as pl
from jax.experimental.pallas import tpu as pltpu
from jax.sharding import PartitionSpec as P

ROWS, D, FF, N = 2560, 7168, 18432, 16
SHARD, F = ROWS // N, FF // N
C = 512
CHUNKS = D // C
PIECES = ((0, 56), (56, 56), (112, 48))
T = 256
TILES = ROWS // T
E = 256
STEPS = D // E
LAG_B, LAG_C, LAG_D, LAG_E = 1, 3, 5, 7
BF, F32 = jnp.bfloat16, jnp.float32
NT = (((1,), (1,)), ((), ()))
TN = (((0,), (0,)), ((), ()))
ANY = pl.BlockSpec(memory_space=pl.ANY)


def dot(a, b, dims=(((1,), (0,)), ((), ()))):
    return lax.dot_general(a, b, dims, preferred_element_type=F32)


def across(device, mask):
    return device + mask * (1 - 2 * lax.rem(lax.div(device, jnp.int32(mask)), jnp.int32(2)))


def axis_mask(i):
    return 8 - 5 * i + i * i


def masks(start):
    i = [lax.rem(jnp.int32(start + k), jnp.int32(3)) for k in range(3)]
    return [axis_mask(k) for k in i]


def loop(lo, hi, body):
    lax.fori_loop(lo, hi, lambda i, c: (body(i), c)[1], 0)


class Gather:
    SEMS = [
        pltpu.SemaphoreType.DMA((3, 3 * CHUNKS)),
        pltpu.SemaphoreType.DMA((CHUNKS,)),
        pltpu.SemaphoreType.DMA((CHUNKS,)),
        pltpu.SemaphoreType.DMA((2,)),
    ]

    def __init__(self, own, g, buf, arrived, paired, sent, loaded):
        self.own_ref, self.g, self.buf = own, g, buf
        self.arrived, self.paired, self.sent, self.loaded = arrived, paired, sent, loaded
        self.me = lax.axis_index("tp").astype(jnp.int32)

    def cols(self, j):
        return pl.ds(pl.multiple_of(j * C, C), C)

    def send(self, j, q, shard, to, phase, src=None):
        rows = pl.ds(*PIECES[q])
        place = self.g.at[shard, rows, self.cols(j)]
        src = place if src is None else src.at[rows, self.cols(j)]
        sem = self.paired.at[j] if phase == 3 else self.arrived.at[phase, 3 * j + q]
        pltpu.make_async_remote_copy(
            src, place, self.sent.at[j], sem, device_id={"tp": to}, device_id_type=pl.DeviceIdType.MESH
        ).start()

    def wait(self, sem, shards, rows):
        ref = self.g.at[pl.ds(0, shards), pl.ds(0, rows), pl.ds(0, C)]
        pltpu.make_async_copy(ref, ref, sem).wait()

    def first(self, j):
        for q in range(3):
            m = masks(j + q)
            for phase in range(3):
                self.send(j, q, self.me, across(self.me, m[phase]), phase, self.own_ref)
            self.send(j, q, self.me, across(self.me, 1), 3, self.own_ref)

    def forward(self, phase, j):
        for q in range(3):
            self.wait(self.arrived.at[phase, 3 * j + q], 2**phase, PIECES[q][1])
            m = masks(j + q)
            shards = [across(self.me, m[phase])]
            for earlier in range(phase):
                shards += [across(s, m[earlier]) for s in shards]
            for s in shards:
                for later in range(phase + 1, 3):
                    self.send(j, q, s, across(self.me, m[later]), later)
                self.send(j, q, s, across(self.me, 1), 3)

    def load(self, j):
        self.wait(self.paired.at[j], 8, SHARD)
        slot = lax.rem(j, 2)
        for r in range(N):
            s = lax.rem(self.me + r, N)
            src = self.own_ref.at[:, self.cols(j)] if r == 0 else self.g.at[s, :, self.cols(j)]
            dst = self.buf.at[slot, pl.ds(pl.multiple_of(s * SHARD, SHARD), SHARD)]
            pltpu.make_async_copy(src, dst, self.loaded.at[slot]).start()

    def pump(self, t):
        def at(lead, f):
            j = t + lead

            @pl.when((j >= 0) & (j < CHUNKS))
            def _():
                f(j)

        at(1, self.load)
        at(2, lambda j: self.forward(2, j))
        at(3, lambda j: self.forward(1, j))
        at(4, lambda j: self.forward(0, j))
        at(7, self.first)

    def start(self):
        for j in range(3):
            self.first(jnp.int32(j))

    def held(self, j):
        slot = lax.rem(j, 2)
        ref = self.buf.at[slot]
        pltpu.make_async_copy(ref, ref, self.loaded.at[slot]).wait()
        return slot

    def finish(self):
        loop(0, CHUNKS, lambda j: self.wait(self.sent.at[j], 15, SHARD))


def wait_like(ref, sem):
    pltpu.make_async_copy(ref, ref, sem).wait()


def hidden_kernel(dy, gate, up, w_down, g, d_out, dw_out, acc, ht, buf, w, o, kept, d, *sems):
    *gs, w_sem, o_sem, kept_sem, d_sem = sems
    ag = Gather(dy, g, buf, *gs)
    ag.start()

    def fetch(i):
        slot = lax.rem(i, 2)
        rows = pl.ds(pl.multiple_of(i * T, T), T)
        pltpu.make_async_copy(gate.at[rows], kept.at[slot, 0], kept_sem.at[slot]).start()
        pltpu.make_async_copy(up.at[rows], kept.at[slot, 1], kept_sem.at[slot]).start()

    def tile(i):
        @pl.when(i + 1 < TILES)
        def _():
            fetch(i + 1)

        slot = lax.rem(i, 2)
        wait_like(kept.at[slot], kept_sem.at[slot])
        return slot, pl.ds(pl.multiple_of(i * T, T), T)

    def w_fetch(j):
        slot = lax.rem(j, 2)
        pltpu.make_async_copy(w_down.at[:, ag.cols(j)], w.at[slot], w_sem.at[slot]).start()

    fetch(jnp.int32(0))
    w_fetch(jnp.int32(0))

    def hide(i):
        slot, rows = tile(i)
        gt, ut = kept[slot, 0].astype(F32), kept[slot, 1].astype(F32)
        h = gt * jax.nn.sigmoid(gt) * ut
        ht[:, rows] = h.T.astype(BF)
        acc[rows, :] = jnp.zeros((T, F), F32)

        @pl.when((lax.rem(i, 2) == 1) & (i < 8))
        def _():
            ag.pump(lax.div(i, 2) - 4)

    loop(0, TILES, hide)

    def chunk(j):
        ag.pump(j)

        @pl.when(j + 1 < CHUNKS)
        def _():
            w_fetch(j + 1)

        slot = ag.held(j)
        wait_like(w.at[slot], w_sem.at[slot])

        def rows_of(i):
            rows = pl.ds(pl.multiple_of(i * T, T), T)
            acc[rows, :] += dot(buf[slot, rows, :], w[slot], NT)

        loop(0, TILES, rows_of)

        @pl.when(j >= 2)
        def _():
            wait_like(o.at[slot], o_sem.at[slot])

        def columns_of(i):
            rows = pl.ds(pl.multiple_of(i * 384, 384), 384)
            o[slot, rows, :] = dot(ht[rows, :], buf[slot]).astype(BF)

        loop(0, F // 384, columns_of)
        pltpu.make_async_copy(o.at[slot], dw_out.at[:, ag.cols(j)], o_sem.at[slot]).start()

    loop(0, CHUNKS, chunk)
    fetch(jnp.int32(0))

    def back(i):
        slot, rows = tile(i)

        @pl.when(i >= 2)
        def _():
            wait_like(d.at[slot], d_sem.at[slot])

        gt, ut, dh = kept[slot, 0].astype(F32), kept[slot, 1].astype(F32), acc[rows, :]
        s = jax.nn.sigmoid(gt)
        d[slot, :, :F] = (dh * ut * (s * (1 + gt * (1 - s)))).astype(BF)
        d[slot, :, F:] = (dh * (gt * s)).astype(BF)
        pltpu.make_async_copy(d.at[slot], d_out.at[rows], d_sem.at[slot]).start()

    loop(0, TILES, back)
    for slot in range(2):
        wait_like(d.at[slot], d_sem.at[slot])
        wait_like(o.at[slot], o_sem.at[slot])
    ag.finish()


def weights_kernel(x, d_in, g, dwg, dwu, buf, d, o, *sems):
    *gs, d_sem, o_sem = sems
    ag = Gather(x, g, buf, *gs)
    ag.start()
    pltpu.make_async_copy(d_in, d, d_sem).start()
    loop(-4, 0, ag.pump)
    wait_like(d, d_sem)

    def chunk(j):
        ag.pump(j)
        slot = ag.held(j)

        @pl.when(j >= 2)
        def _():
            wait_like(o.at[slot], o_sem.at[slot])

        for half in range(2):
            for i in range(C // 256):
                cols = pl.ds(i * 256, 256)
                o[slot, half, cols, :] = dot(buf[slot, :, cols], d[:, pl.ds(half * F, F)], TN).astype(BF)
        rows = pl.ds(pl.multiple_of(j * C, C), C)
        pltpu.make_async_copy(o.at[slot, 0], dwg.at[rows], o_sem.at[slot]).start()
        pltpu.make_async_copy(o.at[slot, 1], dwu.at[rows], o_sem.at[slot]).start()

    loop(0, CHUNKS, chunk)
    for slot in range(2):
        wait_like(o.at[slot], o_sem.at[slot])
    ag.finish()


def sum_kernel(d_in, w_gate, w_up, dx, pair, l1, l2, l3, w, d, sa, sb, sc, sd, se, ab, ac, ad, ae, *sems):
    d_sem, w_sem, pair_sem, r1, r2, r3, send_sem, load_sem, out_sem = sems
    me = lax.axis_index("tp").astype(jnp.int32)
    partner = across(me, 1)
    for half in range(2):
        for r in range(8):
            device = across(me, 1) if half else me
            for bit in (1, 2, 4):
                if r & bit:
                    device = across(device, 2 * bit)
            src = d_in.at[pl.ds(pl.multiple_of(device * SHARD, SHARD), SHARD)]
            pltpu.make_async_copy(src, d.at[pl.ds((half * 8 + r) * SHARD, SHARD)], d_sem).start()

    def w_copies(t):
        rows = pl.ds(pl.multiple_of(t * E, E), E)
        return [
            pltpu.make_async_copy(w_gate.at[rows], w.at[rows, pl.ds(0, F)], w_sem.at[0, t]),
            pltpu.make_async_copy(w_up.at[rows], w.at[rows, pl.ds(F, F)], w_sem.at[1, t]),
        ]

    def w_start(t):
        for c in w_copies(t):
            c.start()

    loop(0, STEPS, w_start)
    wait_like(d, d_sem)

    def part(t, block, blocks=1):
        rows = pl.ds(pl.multiple_of(block * SHARD, SHARD), blocks * SHARD)
        return dot(d[rows, :], w[pl.ds(pl.multiple_of(t * E, E), E), :], NT)

    def send(stage, src, dst, recv, to, slot):
        pltpu.make_async_remote_copy(
            src, dst, send_sem.at[stage, slot], recv, device_id={"tp": to}, device_id_type=pl.DeviceIdType.MESH
        ).start()

    def step(t):
        def at(lag, f):
            u = t - lag

            @pl.when((u >= 0) & (u < STEPS))
            def _():
                m = masks(u)
                f(u, m, [lax.div(k, 2) for k in m])

        def fetch(stage, srcs, buf):
            for k, s in enumerate(srcs):
                pltpu.make_async_copy(s, buf.at[k], load_sem.at[stage]).start()

        def fetch_b(u, m, r):
            wait_like(pair.at[u], pair_sem.at[u])
            fetch(0, [pair.at[u, r[0] + i * r[1] + k * r[2]] for i in range(2) for k in range(2)], ab)

        def fetch_c(u, m, r):
            wait_like(l1.at[u], r1.at[u])
            fetch(1, [pair.at[u, r[1] + k * r[2]] for k in range(2)] + [l1.at[u, 2 + k] for k in range(2)], ac)

        def fetch_d(u, m, r):
            wait_like(l2.at[u], r2.at[u])
            fetch(2, [pair.at[u, r[2]], l1.at[u, 1], l2.at[u, 1]], ad)

        def fetch_e(u, m, r):
            wait_like(l3.at[u], r3.at[u])
            fetch(3, [pair.at[u, 0], l1.at[u, 0], l2.at[u, 0], l3.at[u, 0]], ae)

        at(LAG_B, fetch_b)
        at(LAG_C, fetch_c)
        at(LAG_D, fetch_d)
        at(LAG_E, fetch_e)

        def free(stage, u, src, slot):
            @pl.when(u >= 2)
            def _():
                wait_like(src, send_sem.at[stage, slot])

        def stage_a(u, m, r):
            for c in w_copies(u):
                c.wait()
            slot = lax.rem(u, 2)
            free(0, u, sa.at[slot], slot)
            for k in range(4):
                v = part(u, 8 + 2 * k, 2).astype(BF)
                sa[slot, 2 * k] = v[:SHARD]
                sa[slot, 2 * k + 1] = v[SHARD:]
            send(0, sa.at[slot], pair.at[u], pair_sem.at[u], partner, slot)

        def stage_b(u, m, r):
            slot = lax.rem(u, 2)
            wait_like(ab, load_sem.at[0])
            free(1, u, sb.at[slot], slot)
            for i in range(2):
                for k in range(2):
                    v = part(u, r[0] + i * r[1] + k * r[2]) + ab[2 * i + k].astype(F32)
                    sb[slot, 2 * i + k] = v.astype(BF)
            send(1, sb.at[slot], l1.at[u], r1.at[u], across(me, m[0]), slot)

        def stage_c(u, m, r):
            slot = lax.rem(u, 2)
            wait_like(ac, load_sem.at[1])
            free(2, u, sc.at[slot], slot)
            for k in range(2):
                v = part(u, r[1] + k * r[2]) + ac[k].astype(F32) + ac[2 + k].astype(F32)
                sc[slot, k] = v.astype(BF)
            send(2, sc.at[slot], l2.at[u], r2.at[u], across(me, m[1]), slot)

        def stage_d(u, m, r):
            slot = lax.rem(u, 2)
            wait_like(ad, load_sem.at[2])
            free(3, u, sd.at[slot], slot)
            v = part(u, r[2]) + ad[0].astype(F32) + ad[1].astype(F32) + ad[2].astype(F32)
            sd[slot, 0] = v.astype(BF)
            send(3, sd.at[slot], l3.at[u], r3.at[u], across(me, m[2]), slot)

        def stage_e(u, m, r):
            slot = lax.rem(u, 2)
            wait_like(ae, load_sem.at[3])

            @pl.when(u >= 2)
            def _():
                wait_like(se.at[slot], out_sem.at[slot])

            v = part(u, 0) + ae[0].astype(F32) + ae[1].astype(F32) + ae[2].astype(F32) + ae[3].astype(F32)
            se[slot] = v.astype(BF)
            cols = pl.ds(pl.multiple_of(u * E, E), E)
            pltpu.make_async_copy(se.at[slot], dx.at[:, cols], out_sem.at[slot]).start()

        at(0, stage_a)
        at(LAG_B, stage_b)
        at(LAG_C, stage_c)
        at(LAG_D, stage_d)
        at(LAG_E, stage_e)

    loop(0, STEPS + LAG_E, step)
    for slot in range(2):
        for stage, ref in enumerate((sa, sb, sc, sd)):
            wait_like(ref.at[slot], send_sem.at[stage, slot])
        wait_like(se.at[slot], out_sem.at[slot])


def call(kernel, outs, scratch, flops, args):
    moved = sum(a.size * a.dtype.itemsize for a in (*args, *outs))
    return pl.pallas_call(
        kernel,
        out_shape=outs,
        in_specs=[ANY] * len(args),
        out_specs=[ANY] * len(outs),
        scratch_shapes=scratch,
        cost_estimate=pl.CostEstimate(flops=flops, bytes_accessed=moved, transcendentals=0),
        compiler_params=pltpu.CompilerParams(has_side_effects=True, vmem_limit_bytes=60 * 2**20),
    )(*args)


def solution(mesh):
    sds = jax.ShapeDtypeStruct
    dma = pltpu.SemaphoreType.DMA
    product = 2 * ROWS * D * F

    def step(x, dy, gate, up, w_gate, w_up, w_down):
        _, d, dw_down = call(
            hidden_kernel,
            [sds((N, SHARD, D), BF), sds((ROWS, 2 * F), BF), sds((F, D), BF)],
            [
                pltpu.VMEM((ROWS, F), F32),
                pltpu.VMEM((F, ROWS), BF),
                pltpu.VMEM((2, ROWS, C), BF),
                pltpu.VMEM((2, F, C), BF),
                pltpu.VMEM((2, F, C), BF),
                pltpu.VMEM((2, 2, T, F), BF),
                pltpu.VMEM((2, T, 2 * F), BF),
                *Gather.SEMS,
                dma((2,)),
                dma((2,)),
                dma((2,)),
                dma((2,)),
            ],
            2 * product,
            (dy, gate, up, w_down),
        )
        dx, *_ = call(
            sum_kernel,
            [sds((SHARD, D), BF)] + [sds((STEPS, n, SHARD, E), BF) for n in (8, 4, 2, 1)],
            [
                pltpu.VMEM((D, 2 * F), BF),
                pltpu.VMEM((ROWS, 2 * F), BF),
                *[pltpu.VMEM((2, n, SHARD, E), BF) for n in (8, 4, 2, 1)],
                pltpu.VMEM((2, SHARD, E), BF),
                *[pltpu.VMEM((n, SHARD, E), BF) for n in (4, 4, 3, 4)],
                dma,
                dma((2, STEPS)),
                dma((STEPS,)),
                dma((STEPS,)),
                dma((STEPS,)),
                dma((STEPS,)),
                dma((4, 2)),
                dma((4,)),
                dma((2,)),
            ],
            2 * product,
            (d, w_gate, w_up),
        )
        _, dw_gate, dw_up = call(
            weights_kernel,
            [sds((N, SHARD, D), BF), sds((D, F), BF), sds((D, F), BF)],
            [
                pltpu.VMEM((2, ROWS, C), BF),
                pltpu.VMEM((ROWS, 2 * F), BF),
                pltpu.VMEM((2, 2, C, F), BF),
                *Gather.SEMS,
                dma,
                dma((2,)),
            ],
            2 * product,
            (x, d),
        )
        return dx, dw_gate, dw_up, dw_down

    rows, cols = P(("dp", "tp"), None), P("dp", "tp")
    weight, down = P(None, "tp"), P("tp", None)
    return jax.shard_map(
        step,
        mesh=mesh,
        in_specs=(rows, rows, cols, cols, weight, weight, down),
        out_specs=(rows, cols, cols, rows),
        check_vma=False,
    )
```

time: 1780 us -> 586 us (0.33)
  starting transfers between devices: 719 us -> 0 us
  Pallas kernels: 0 us -> 548 us
  waiting for transfers between devices: 474 us -> 0 us
  matrix products: 389 us -> 0 us
  other arithmetic: 109 us -> 0.01 us
    dot_general x34 -> x0, starting transfers between devices: 719 us -> none  [step(): dx = jnp.dot(d_gate, w_gate.T) + jnp.dot(d_up, w_up.T)]
    pallas_call x0 -> x3, Pallas kernels: none -> 548 us  [call(): pl.pallas_call(kernel, out_shape=outs, in_specs=[ANY] * len(args), out_sp...]
    dot_general x20 -> x0, matrix products: 389 us -> none  [the longest x3 160 us: by_group(): jnp.einsum('gta,gtb->gab', a, b, preferred_element_type=jnp.float32)]
    dot_general x34 -> x0, waiting for transfers between devices: 327 us -> none  [step(): dx = jnp.dot(d_gate, w_gate.T) + jnp.dot(d_up, w_up.T)]
    unnamed x4 -> x0, waiting for transfers between devices: 147 us -> none
    dot_general x32 -> x0, other arithmetic: 104 us -> none  [the longest x16 72.9 us: step(): dx = jnp.dot(d_gate, w_gate.T) + jnp.dot(d_up, w_up.T)]
    unnamed x10 -> x14, local copies, waits for them, and re-layouts: 44.6 us -> 36.7 us
  transfers between devices with their start and end apart: 36 -> 0, of which waited for: 19 -> 0; matrix products, arithmetic and copies ran while one was open for 30% -> 0% of each run, Pallas kernels for 0% -> 0%
where the time goes in v1:
time: 586 us; the launch traced here: 585 us
  Pallas kernels  548 us (94%)
  local copies, waits for them, and re-layouts  36.7 us (6%)
    pallas_call x3, Pallas kernels, call(): pl.pallas_call(kernel, out_shape=outs, in_specs=[ANY] * len(args), out_sp...  548 us
    unnamed x14, local copies, waits for them, and re-layouts  36.7 us

profile of v1, /device:TPU:0, one launch (start us, length us, event | category | flops | bytes accessed | tf_op | source)
XLA Modules:
  0.0 584.9 jit_solution(4548987172795306040)
XLA Ops:
  0.6 195.7 %shard_map.102 = (bf16[16,160,7168]{2,1,0:T(8,128)(2,1)}, bf16[2560,2304]{1,0:T(8,128)(2,1)}, bf16[1152,7168]{1,0:T(8,128)(2,1)}) custom-call(bf16[160,7168]{1,0:T(8,128)(2,1)} %dy.1, bf16[2560,1152]{1,0:T(8,128)(2,1)} %gate.1, bf16[2560,1152]{1,0:T(8,128)(2,1)} %up.1, bf16[1152,7168]{1,0:T(8,128)(2,1)} %w_down.1), custom_call_target="tpu_custom_call" | custom-call | flops 84557168640 | bytes 95617024 | tf_op jit(solution)/shard_map/pallas_call | solution.py:395
  196.4 155.2 %shard_map.104 = (bf16[16,160,7168]{2,1,0:T(8,128)(2,1)}, bf16[7168,1152]{1,0:T(8,128)(2,1)}, bf16[7168,1152]{1,0:T(8,128)(2,1)}) custom-call(bf16[160,7168]{1,0:T(8,128)(2,1)} %x.1, bf16[2560,2304]{1,0:T(8,128)(2,1)} %get-tuple-element.9.d_in), custom_call_target="tpu_custom_call" | custom-call | flops 84557168640 | bytes 83820544 | tf_op jit(solution)/shard_map/pallas_call | solution.py:395
  351.6 196.6 %shard_map.103 = (bf16[160,7168]{1,0:T(8,128)(2,1)}, bf16[28,8,160,256]{3,2,1,0:T(8,128)(2,1)}, bf16[28,4,160,256]{3,2,1,0:T(8,128)(2,1)}, bf16[28,2,160,256]{3,2,1,0:T(8,128)(2,1)}, bf16[28,1,160,256]{3,2,1,0:T(8,128)(2,1)}) custom-call(bf16[2560,2304]{1,0:T(8,128)(2,1)} %get-tuple-element.9.d_in, bf16[7168,1152]{1,0:T(8,128)(2,1)} %w_gate.1, ...), custom_call_target="tpu_custom_call" | custom-call | flops 84557168640 | bytes 81526784 | tf_op jit(solution)/shard_map/pallas_call | solution.py:395
  548.2 3.2 copy.15
  551.4 0.0 copy-start
  551.4 0.0 slice-start
  551.4 0.0 slice-start.1
  551.4 16.4 %copy.16 = bf16[7168,1152]{1,0:T(8,128)(2,1)} copy(bf16[7168,1152]{1,0:T(8,128)(2,1)} %get-tuple-element.19) | data formatting | bytes 33030144
  567.8 0.0 copy-done
  567.8 0.0 slice-start.2
  567.8 0.0 slice-start.3
  567.8 8.4 %copy.17 = bf16[7168,1152]{1,0:T(8,128)(2,1)} copy(bf16[7168,1152]{1,0:T(8,128)(2,1)S(1)} %copy-done) | data formatting | bytes 33030144
  576.2 0.0 slice-done
  576.2 0.0 slice-done.1
  576.2 1.5 slice-done.2
  577.8 1.1 slice-done.3
  578.9 6.1 %copy.18 = bf16[1152,7168]{1,0:T(8,128)(2,1)} copy(bf16[1152,7168]{1,0:T(8,128)(2,1)S(1)} %bitcast.1) | data formatting | bytes 33030144
  (1 shorter events, 0.0 us)
Async XLA Ops:
  551.4 16.4 %copy-start = (bf16[7168,1152]{1,0:T(8,128)(2,1)S(1)}, bf16[7168,1152]{1,0:T(8,128)(2,1)}, u32[]{:S(2)}) copy-start(bf16[7168,1152]{1,0:T(8,128)(2,1)} %get-tuple-element.20) | copy-start | bytes 49545220
  551.4 24.8 %slice-start = ((s8[16515072]{0:T(1024)(128)(4,1)}), s8[4194304]{0:T(1024)(128)(4,1)S(1)}, s32[]{:S(2)}) async-start(s8[16515072]{0:T(1024)(128)(4,1)} %bitcast), calls=%async_computation | async-start | bytes 8388608
  551.4 24.8 %slice-start.1 = ((s8[16515072]{0:T(1024)(128)(4,1)}), s8[4194304]{0:T(1024)(128)(4,1)S(1)}, s32[]{:S(2)}) async-start(s8[16515072]{0:T(1024)(128)(4,1)} %bitcast), calls=%async_computation.1 | async-start | bytes 8388608
  567.8 9.9 %slice-start.2 = ((s8[16515072]{0:T(1024)(128)(4,1)}), s8[4194304]{0:T(1024)(128)(4,1)S(1)}, s32[]{:S(2)}) async-start(s8[16515072]{0:T(1024)(128)(4,1)} %bitcast), calls=%async_computation.2 | async-start | bytes 8388608
  567.8 11.0 %slice-start.3 = ((s8[16515072]{0:T(1024)(128)(4,1)}), s8[3932160]{0:T(1024)(128)(4,1)S(1)}, s32[]{:S(2)}) async-start(s8[16515072]{0:T(1024)(128)(4,1)} %bitcast), calls=%async_computation.3 | async-start | bytes 7864320

commit v2 on v0

v2 whole, which is shorter than its diff:
```python
import jax
import jax.numpy as jnp
from jax import lax
from jax.experimental import pallas as pl
from jax.experimental.pallas import tpu as pltpu
from jax.sharding import PartitionSpec as P

ROWS, D, FF, N = 2560, 7168, 18432, 16
SHARD, F = ROWS // N, FF // N
CY, CX = 512, 256
CHUNKS = D // CY
PIECES = ((0, 56), (56, 56), (112, 48))
T = 256
TILES = ROWS // T
E = 256
STEPS = D // E
LAG_B, LAG_C, LAG_D, LAG_E = 1, 3, 5, 7
LAG_X = 3
LEADS_X = (10, 6, 2, 16)
X_FROM = 8
BF, F32 = jnp.bfloat16, jnp.float32
NT = (((1,), (1,)), ((), ()))
TN = (((0,), (0,)), ((), ()))
ANY = pl.BlockSpec(memory_space=pl.ANY)


def dot(a, b, dims=(((1,), (0,)), ((), ()))):
    return lax.dot_general(a, b, dims, preferred_element_type=F32)


def across(device, mask):
    return device + mask * (1 - 2 * lax.rem(lax.div(device, jnp.int32(mask)), jnp.int32(2)))


def axis_mask(i):
    return 8 - 5 * i + i * i


def masks(start):
    i = [lax.rem(jnp.int32(start + k), jnp.int32(3)) for k in range(3)]
    return [axis_mask(k) for k in i]


def loop(lo, hi, body):
    lax.fori_loop(lo, hi, lambda i, c: (body(i), c)[1], 0)


class Gather:
    @staticmethod
    def sems(c):
        n = D // c
        return [pltpu.SemaphoreType.DMA(s) for s in ((3, 3 * n), (n,), (n,), (2,))]

    def __init__(self, own, g, buf, c, leads, place, arrived, paired, sent, loaded):
        self.own_ref, self.g, self.buf, self.c, self.leads, self.place = own, g, buf, c, leads, place
        self.arrived, self.paired, self.sent, self.loaded = arrived, paired, sent, loaded
        self.me = lax.axis_index("tp").astype(jnp.int32)
        self.chunks = D // c

    def cols(self, j):
        return pl.ds(pl.multiple_of(j * self.c, self.c), self.c)

    def send(self, j, q, shard, to, phase, src=None):
        rows = pl.ds(*PIECES[q])
        place = self.g.at[shard, rows, self.cols(j)]
        src = place if src is None else src.at[rows, self.cols(j)]
        sem = self.paired.at[j] if phase == 3 else self.arrived.at[phase, 3 * j + q]
        pltpu.make_async_remote_copy(
            src, place, self.sent.at[j], sem, device_id={"tp": to}, device_id_type=pl.DeviceIdType.MESH
        ).start()

    def wait(self, sem, shards, rows):
        ref = self.g.at[pl.ds(0, shards), pl.ds(0, rows), pl.ds(0, self.c)]
        pltpu.make_async_copy(ref, ref, sem).wait()

    def first(self, j):
        for q in range(3):
            m = masks(j + q)
            for phase in range(3):
                self.send(j, q, self.me, across(self.me, m[phase]), phase, self.own_ref)
            self.send(j, q, self.me, across(self.me, 1), 3, self.own_ref)

    def forward(self, phase, j):
        for q in range(3):
            self.wait(self.arrived.at[phase, 3 * j + q], 2**phase, PIECES[q][1])
            m = masks(j + q)
            shards = [across(self.me, m[phase])]
            for earlier in range(phase):
                shards += [across(s, m[earlier]) for s in shards]
            for s in shards:
                for later in range(phase + 1, 3):
                    self.send(j, q, s, across(self.me, m[later]), later)
                self.send(j, q, s, across(self.me, 1), 3)

    def load(self, j):
        self.wait(self.paired.at[j], 8, SHARD)
        slot = lax.rem(j, 2)
        for r in range(N):
            device, at = self.place(r)
            src = self.own_ref.at[:, self.cols(j)] if r == 0 else self.g.at[device, :, self.cols(j)]
            dst = self.buf.at[slot, pl.ds(pl.multiple_of(at * SHARD, SHARD), SHARD)]
            pltpu.make_async_copy(src, dst, self.loaded.at[slot]).start()

    def guarded(self, j, f):
        @pl.when((j >= 0) & (j < self.chunks))
        def _():
            f(j)

    def pump(self, t):
        for phase in (2, 1, 0):
            self.guarded(t + self.leads[phase], lambda j: self.forward(phase, j))
        self.guarded(t + self.leads[3], self.first)

    def held(self, j):
        slot = lax.rem(j, 2)
        ref = self.buf.at[slot]
        pltpu.make_async_copy(ref, ref, self.loaded.at[slot]).wait()
        return slot

    def finish(self):
        loop(0, self.chunks, lambda j: self.wait(self.sent.at[j], 15, SHARD))


def wait_like(ref, sem):
    pltpu.make_async_copy(ref, ref, sem).wait()


def relative(me, p):
    device = across(me, 1) if p >= 8 else me
    for bit in (1, 2, 4):
        if p & bit:
            device = across(device, 2 * bit)
    return device


def kernel(*refs):
    it = iter(refs)
    take = lambda n: [next(it) for _ in range(n)]
    x, dy, gate, up, w_gate, w_up, w_down = take(7)
    dx, dwg, dwu, dwd, gy, gx, pair, l1, l2, l3 = take(10)
    d, acc, ht, ybuf, wd, o, kept = take(7)
    w, xbuf, sa, sb, sc, sd, se, ab, ac, ad, ae = take(11)
    y_sems, x_sems = take(4), take(4)
    wd_sem, o_sem, kept_sem, ox_sem = take(4)
    w_sem, pair_sem, r1, r2, r3, send_sem, load_sem, out_sem = take(8)
    me = lax.axis_index("tp").astype(jnp.int32)
    partner = across(me, 1)

    def absolute(r):
        s = lax.rem(me + r, jnp.int32(N))
        return s, s

    y = Gather(dy, gy, ybuf, CY, (4, 3, 2, 7), absolute, *y_sems)
    xg = Gather(x, gx, xbuf, CX, LEADS_X, lambda p: (relative(me, p), p), *x_sems)

    for j in range(3):
        y.first(jnp.int32(j))

    def fetch(slot, start, rows):
        span = pl.ds(start, rows)
        for k, ref in enumerate((gate, up)):
            pltpu.make_async_copy(ref.at[span], kept.at[slot, k, pl.ds(0, rows)], kept_sem.at[slot]).start()

    def fetched(slot, rows):
        wait_like(kept.at[slot, :, pl.ds(0, rows)], kept_sem.at[slot])
        return [kept[slot, k, :rows].astype(F32) for k in range(2)]

    def wd_fetch(j):
        slot = lax.rem(j, 2)
        pltpu.make_async_copy(w_down.at[:, y.cols(j)], wd.at[slot], wd_sem.at[slot]).start()

    fetch(0, 0, T)
    wd_fetch(jnp.int32(0))

    def hide(i):
        slot, rows = lax.rem(i, 2), pl.ds(pl.multiple_of(i * T, T), T)

        @pl.when(i + 1 < TILES)
        def _():
            fetch(1 - slot, pl.multiple_of((i + 1) * T, T), T)

        gt, ut = fetched(slot, T)
        ht[:, rows] = (gt * jax.nn.sigmoid(gt) * ut).T.astype(BF)
        acc[rows, :] = jnp.zeros((T, F), F32)

        @pl.when((lax.rem(i, 2) == 1) & (i < 8))
        def _():
            t = lax.div(i, 2) - 4
            y.guarded(t + 1, y.load)
            y.pump(t)

    loop(0, TILES, hide)

    def chunk(j):
        y.guarded(j + 1, y.load)
        y.pump(j)

        @pl.when(j >= X_FROM)
        def _():
            for k in range(2):
                xg.pump(2 * (j - X_FROM) - LEADS_X[3] + k)

        @pl.when(j + 1 < CHUNKS)
        def _():
            wd_fetch(j + 1)

        slot = y.held(j)
        wait_like(wd.at[slot], wd_sem.at[slot])

        def rows_of(i):
            rows = pl.ds(pl.multiple_of(i * (ROWS // 2), ROWS // 2), ROWS // 2)
            acc[rows, :] += dot(ybuf[slot, rows, :], wd[slot], NT)

        loop(0, 2, rows_of)

        @pl.when(j >= 2)
        def _():
            wait_like(o.at[slot], o_sem.at[slot])

        o[slot] = dot(ht[...], ybuf[slot]).astype(BF)
        pltpu.make_async_copy(o.at[slot], dwd.at[:, y.cols(j)], o_sem.at[slot]).start()

    loop(0, CHUNKS, chunk)

    sent_x = 2 * (CHUNKS - X_FROM) - LEADS_X[3]
    fetch(0, pl.multiple_of(me * SHARD, SHARD), SHARD)
    for p in range(N):
        slot, start = p % 2, pl.multiple_of(relative(me, p) * SHARD, SHARD)
        if p + 1 < N:
            fetch(1 - slot, pl.multiple_of(relative(me, p + 1) * SHARD, SHARD), SHARD)
        gt, ut = fetched(slot, SHARD)
        dh, s = acc[pl.ds(start, SHARD), :], jax.nn.sigmoid(gt)
        rows = pl.ds(p * SHARD, SHARD)
        d[rows, :F] = (dh * ut * (s * (1 + gt * (1 - s)))).astype(BF)
        d[rows, F:] = (dh * (gt * s)).astype(BF)
        if p % 3 == 2:
            xg.pump(jnp.int32(sent_x + p // 3))
    pumped = sent_x + N // 3

    def w_start(t):
        rows, slot = pl.ds(pl.multiple_of(t * E, E), E), lax.rem(t, 3)
        for k, ref in enumerate((w_gate, w_up)):
            pltpu.make_async_copy(ref.at[rows], w.at[slot, :, pl.ds(k * F, F)], w_sem.at[slot]).start()

    def part(t, half):
        return dot(d[pl.ds(half * (ROWS // 2), ROWS // 2), :], w[lax.rem(t, 3)], NT)

    def held(u, block):
        slot = lax.rem(u, 8)
        row = lax.rem(slot, 2) * (ROWS // 2) + block * SHARD
        col = pl.multiple_of(lax.div(slot, 2) * E, E)
        return pl.ds(pl.multiple_of(row, SHARD), SHARD), pl.ds(col, E)

    def send(stage, src, dst, recv, to, slot):
        pltpu.make_async_remote_copy(
            src, dst, send_sem.at[stage, slot], recv, device_id={"tp": to}, device_id_type=pl.DeviceIdType.MESH
        ).start()

    def free(stage, u, src, slot):
        @pl.when(u >= 2)
        def _():
            wait_like(src, send_sem.at[stage, slot])

    def step(t):
        def at(lag, f):
            u = t - lag

            @pl.when((u >= 0) & (u < STEPS))
            def _():
                m = masks(u)
                f(u, m, [lax.div(k, 2) for k in m])

        def get(stage, srcs, buf):
            for k, s in enumerate(srcs):
                pltpu.make_async_copy(s, buf.at[k], load_sem.at[stage]).start()

        def get_b(u, m, r):
            wait_like(pair.at[u], pair_sem.at[u])
            pltpu.make_async_copy(pair.at[u], ab, load_sem.at[0]).start()

        def get_c(u, m, r):
            wait_like(l1.at[u], r1.at[u])
            get(1, [l1.at[u, 2 + k] for k in range(2)], ac)

        def get_d(u, m, r):
            wait_like(l2.at[u], r2.at[u])
            get(2, [l1.at[u, 1], l2.at[u, 1]], ad)

        def get_e(u, m, r):
            wait_like(l3.at[u], r3.at[u])
            get(3, [l1.at[u, 0], l2.at[u, 0], l3.at[u, 0]], ae)

        def stage_a(u, m, r):
            wait_like(w.at[lax.rem(u, 3)], w_sem.at[lax.rem(u, 3)])
            slot = lax.rem(u, 2)
            free(0, u, sa.at[slot], slot)
            sa[slot] = part(u, 1).astype(BF)
            send(0, sa.at[slot], pair.at[u], pair_sem.at[u], partner, slot)

        def stage_b(u, m, r):
            slot = lax.rem(u, 2)
            wait_like(ab, load_sem.at[0])
            free(1, u, sb.at[slot], slot)
            row, col = held(u, 0)
            acc[pl.ds(row.start, ROWS // 2), col] = part(u, 0) + ab[...].astype(F32)
            for i in range(2):
                for k in range(2):
                    sb[slot, 2 * i + k] = acc[held(u, r[0] + i * r[1] + k * r[2])].astype(BF)
            send(1, sb.at[slot], l1.at[u], r1.at[u], across(me, m[0]), slot)

        def stage_c(u, m, r):
            slot = lax.rem(u, 2)
            wait_like(ac, load_sem.at[1])
            free(2, u, sc.at[slot], slot)
            for k in range(2):
                sc[slot, k] = (acc[held(u, r[1] + k * r[2])] + ac[k].astype(F32)).astype(BF)
            send(2, sc.at[slot], l2.at[u], r2.at[u], across(me, m[1]), slot)

        def stage_d(u, m, r):
            slot = lax.rem(u, 2)
            wait_like(ad, load_sem.at[2])
            free(3, u, sd.at[slot], slot)
            sd[slot, 0] = (acc[held(u, r[2])] + ad[0].astype(F32) + ad[1].astype(F32)).astype(BF)
            send(3, sd.at[slot], l3.at[u], r3.at[u], across(me, m[2]), slot)

        def stage_e(u, m, r):
            slot = lax.rem(u, 2)
            wait_like(ae, load_sem.at[3])

            @pl.when(u >= 2)
            def _():
                wait_like(se.at[slot], out_sem.at[slot])

            v = acc[held(u, 0)] + ae[0].astype(F32) + ae[1].astype(F32) + ae[2].astype(F32)
            se[slot] = v.astype(BF)
            pltpu.make_async_copy(se.at[slot], dx.at[:, pl.ds(pl.multiple_of(u * E, E), E)], out_sem.at[slot]).start()

        def weights(u, m, r):
            slot = xg.held(u)

            @pl.when(u >= 2)
            def _():
                wait_like(kept.at[slot], ox_sem.at[slot])

            v = dot(xbuf[slot], d[...], TN)
            rows = pl.ds(pl.multiple_of(u * CX, CX), CX)
            for k, ref in enumerate((dwg, dwu)):
                kept[slot, k] = v[:, k * F : (k + 1) * F].astype(BF)
                pltpu.make_async_copy(kept.at[slot, k], ref.at[rows], ox_sem.at[slot]).start()

        @pl.when(t + 1 < STEPS)
        def _():
            w_start(t + 1)

        at(LAG_X - 1, lambda u, m, r: xg.load(u))
        at(LAG_B, get_b)
        at(LAG_C, get_c)
        at(LAG_D, get_d)
        at(LAG_E, get_e)
        at(0, stage_a)
        at(LAG_B, stage_b)
        at(LAG_C, stage_c)
        at(LAG_D, stage_d)
        at(LAG_E, stage_e)
        xg.pump(t + pumped)
        at(LAG_X, weights)

    w_start(jnp.int32(0))
    loop(0, STEPS + max(LAG_E, LAG_X), step)
    for slot in range(2):
        for stage, ref in enumerate((sa, sb, sc, sd)):
            wait_like(ref.at[slot], send_sem.at[stage, slot])
        wait_like(se.at[slot], out_sem.at[slot])
        wait_like(o.at[slot], o_sem.at[slot])
        wait_like(kept.at[slot], ox_sem.at[slot])
    y.finish()
    xg.finish()


def solution(mesh):
    sds, vmem = jax.ShapeDtypeStruct, lambda *s: pltpu.VMEM(s, BF)
    dma = pltpu.SemaphoreType.DMA

    def step(*args):
        outs = [sds((SHARD, D), BF), sds((D, F), BF), sds((D, F), BF), sds((F, D), BF)]
        outs += [sds((N, SHARD, D), BF)] * 2
        outs += [sds((STEPS, ROWS // 2, E), BF)] + [sds((STEPS, n, SHARD, E), BF) for n in (4, 2, 1)]
        return pl.pallas_call(
            kernel,
            out_shape=outs,
            in_specs=[ANY] * len(args),
            out_specs=[ANY] * len(outs),
            scratch_shapes=[
                vmem(ROWS, 2 * F),
                pltpu.VMEM((ROWS, F), F32),
                vmem(F, ROWS),
                vmem(2, ROWS, CY),
                vmem(2, F, CY),
                vmem(2, F, CY),
                vmem(2, 2, T, F),
                vmem(3, E, 2 * F),
                vmem(2, ROWS, CX),
                vmem(2, ROWS // 2, E),
                *[vmem(2, n, SHARD, E) for n in (4, 2, 1)],
                vmem(2, SHARD, E),
                vmem(ROWS // 2, E),
                *[vmem(n, SHARD, E) for n in (2, 2, 3)],
                *Gather.sems(CY),
                *Gather.sems(CX),
                *[dma((2,))] * 4,
                dma((3,)),
                *[dma((STEPS,))] * 4,
                dma((4, 2)),
                dma((4,)),
                dma((2,)),
            ],
            cost_estimate=pl.CostEstimate(flops=12 * ROWS * D * F, bytes_accessed=400 * 2**20, transcendentals=0),
            compiler_params=pltpu.CompilerParams(has_side_effects=True, vmem_limit_bytes=63 * 2**20),
        )(*args)[:4]

    rows, cols = P(("dp", "tp"), None), P("dp", "tp")
    weight, down = P(None, "tp"), P("tp", None)
    return jax.shard_map(
        step,
        mesh=mesh,
        in_specs=(rows, rows, cols, cols, weight, weight, down),
        out_specs=(rows, cols, cols, rows),
        check_vma=False,
    )
```

time: 1780 us -> 458 us (0.26)
  starting transfers between devices: 719 us -> 0 us
  waiting for transfers between devices: 474 us -> 0 us
  Pallas kernels: 0 us -> 419 us
  matrix products: 389 us -> 0 us
  other arithmetic: 109 us -> 0.01 us
    dot_general x34 -> x0, starting transfers between devices: 719 us -> none  [step(): dx = jnp.dot(d_gate, w_gate.T) + jnp.dot(d_up, w_up.T)]
    pallas_call x0 -> x1, Pallas kernels: none -> 419 us  [step(): pl.pallas_call(kernel, out_shape=outs, in_specs=[ANY] * len(args), out_sp...]
    dot_general x20 -> x0, matrix products: 389 us -> none  [the longest x3 160 us: by_group(): jnp.einsum('gta,gtb->gab', a, b, preferred_element_type=jnp.float32)]
    dot_general x34 -> x0, waiting for transfers between devices: 327 us -> none  [step(): dx = jnp.dot(d_gate, w_gate.T) + jnp.dot(d_up, w_up.T)]
    unnamed x4 -> x0, waiting for transfers between devices: 147 us -> none
    dot_general x32 -> x0, other arithmetic: 104 us -> none  [the longest x16 72.9 us: step(): dx = jnp.dot(d_gate, w_gate.T) + jnp.dot(d_up, w_up.T)]
    unnamed x10 -> x14, local copies, waits for them, and re-layouts: 44.6 us -> 36.7 us
  transfers between devices with their start and end apart: 36 -> 0, of which waited for: 19 -> 0; matrix products, arithmetic and copies ran while one was open for 30% -> 0% of each run, Pallas kernels for 0% -> 0%
where the time goes in v2:
time: 458 us; the launch traced here: 457 us
  Pallas kernels  419 us (91%)
  local copies, waits for them, and re-layouts  36.7 us (8%)
    pallas_call x1, Pallas kernels, step(): pl.pallas_call(kernel, out_shape=outs, in_specs=[ANY] * len(args), out_sp...  419 us
    unnamed x14, local copies, waits for them, and re-layouts  36.7 us

profile of v2, /device:TPU:0, one launch (start us, length us, event | category | flops | bytes accessed | tf_op | source)
XLA Modules:
  0.0 456.7 jit_solution(7784393521299669512)
XLA Ops:
  0.6 419.3 %shard_map.102 = (bf16[160,7168]{1,0:T(8,128)(2,1)}, bf16[7168,1152]{1,0:T(8,128)(2,1)}, bf16[7168,1152]{1,0:T(8,128)(2,1)}, bf16[1152,7168]{1,0:T(8,128)(2,1)},...) custom-call(bf16[160,7168]{1,0:T(8,128)(2,1)} %refs_0_.1, ...), custom_call_target="tpu_custom_call" | custom-call | flops 253671505920 | bytes 419430400 | tf_op jit(solution)/shard_map/pallas_call | solution.py:388
  420.0 3.2 copy.15
  423.1 0.0 copy-start
  423.1 0.0 slice-start
  423.1 0.0 slice-start.1
  423.1 16.4 %copy.16 = bf16[7168,1152]{1,0:T(8,128)(2,1)} copy(bf16[7168,1152]{1,0:T(8,128)(2,1)} %get-tuple-element.17) | data formatting | bytes 33030144
  439.6 0.0 copy-done
  439.6 0.0 slice-start.2
  439.6 0.0 slice-start.3
  439.6 8.4 %copy.17 = bf16[7168,1152]{1,0:T(8,128)(2,1)} copy(bf16[7168,1152]{1,0:T(8,128)(2,1)S(1)} %copy-done) | data formatting | bytes 33030144
  448.0 0.0 slice-done
  448.0 0.0 slice-done.1
  448.0 1.5 slice-done.2
  449.5 1.1 slice-done.3
  450.6 6.1 %copy.18 = bf16[1152,7168]{1,0:T(8,128)(2,1)} copy(bf16[1152,7168]{1,0:T(8,128)(2,1)S(1)} %bitcast.1) | data formatting | bytes 33030144
  (1 shorter events, 0.0 us)
Async XLA Ops:
  423.1 16.4 %copy-start = (bf16[7168,1152]{1,0:T(8,128)(2,1)S(1)}, bf16[7168,1152]{1,0:T(8,128)(2,1)}, u32[]{:S(2)}) copy-start(bf16[7168,1152]{1,0:T(8,128)(2,1)} %get-tuple-element.18) | copy-start | bytes 49545220
  423.1 24.8 %slice-start = ((s8[16515072]{0:T(1024)(128)(4,1)}), s8[4194304]{0:T(1024)(128)(4,1)S(1)}, s32[]{:S(2)}) async-start(s8[16515072]{0:T(1024)(128)(4,1)} %bitcast), calls=%async_computation | async-start | bytes 8388608
  423.1 24.8 %slice-start.1 = ((s8[16515072]{0:T(1024)(128)(4,1)}), s8[4194304]{0:T(1024)(128)(4,1)S(1)}, s32[]{:S(2)}) async-start(s8[16515072]{0:T(1024)(128)(4,1)} %bitcast), calls=%async_computation.1 | async-start | bytes 8388608
  439.6 9.9 %slice-start.2 = ((s8[16515072]{0:T(1024)(128)(4,1)}), s8[4194304]{0:T(1024)(128)(4,1)S(1)}, s32[]{:S(2)}) async-start(s8[16515072]{0:T(1024)(128)(4,1)} %bitcast), calls=%async_computation.2 | async-start | bytes 8388608
  439.6 11.0 %slice-start.3 = ((s8[16515072]{0:T(1024)(128)(4,1)}), s8[3932160]{0:T(1024)(128)(4,1)S(1)}, s32[]{:S(2)}) async-start(s8[16515072]{0:T(1024)(128)(4,1)} %bitcast), calls=%async_computation.3 | async-start | bytes 7864320

commit v3 on v2

--- a/solution.py
+++ b/solution.py
@@ -7,16 +7,20 @@
 
 ROWS, D, FF, N = 2560, 7168, 18432, 16
 SHARD, F = ROWS // N, FF // N
-CY, CX = 512, 256
-CHUNKS = D // CY
-PIECES = ((0, 56), (56, 56), (112, 48))
+C = 256
+CW = 512
+CHUNKS = D // CW
 T = 256
 TILES = ROWS // T
 E = 256
 STEPS = D // E
 LAG_B, LAG_C, LAG_D, LAG_E = 1, 3, 5, 7
-LAG_X = 3
-LEADS_X = (10, 6, 2, 16)
+LAG_X = 1
+LATE = 8
+EARLY = D // C - LATE
+HELD = 6
+LEADS_Y = (8, 6, 4, 12)
+LEADS_X = (11, 6, 2, 16)
 X_FROM = 8
 BF, F32 = jnp.bfloat16, jnp.float32
 NT = (((1,), (1,)), ((), ()))
@@ -46,63 +50,67 @@
 
 
 class Gather:
-    @staticmethod
-    def sems(c):
-        n = D // c
-        return [pltpu.SemaphoreType.DMA(s) for s in ((3, 3 * n), (n,), (n,), (2,))]
-
-    def __init__(self, own, g, buf, c, leads, place, arrived, paired, sent, loaded):
-        self.own_ref, self.g, self.buf, self.c, self.leads, self.place = own, g, buf, c, leads, place
+    CHUNKS = D // C
+    SEMS = [pltpu.SemaphoreType.DMA(s) for s in ((3, CHUNKS), (CHUNKS,), (CHUNKS,), (2,))]
+
+    def __init__(self, own, g, buf, leads, relative, arrived, paired, sent, loaded):
+        self.own_ref, self.g, self.buf, self.leads, self.relative = own, g, buf, leads, relative
         self.arrived, self.paired, self.sent, self.loaded = arrived, paired, sent, loaded
         self.me = lax.axis_index("tp").astype(jnp.int32)
-        self.chunks = D // c
-
-    def cols(self, j):
-        return pl.ds(pl.multiple_of(j * self.c, self.c), self.c)
-
-    def send(self, j, q, shard, to, phase, src=None):
-        rows = pl.ds(*PIECES[q])
-        place = self.g.at[shard, rows, self.cols(j)]
-        src = place if src is None else src.at[rows, self.cols(j)]
-        sem = self.paired.at[j] if phase == 3 else self.arrived.at[phase, 3 * j + q]
+        self.width = buf.shape[-1] // C
+
+    def send(self, j, src, half, r, to, sem):
         pltpu.make_async_remote_copy(
-            src, place, self.sent.at[j], sem, device_id={"tp": to}, device_id_type=pl.DeviceIdType.MESH
+            src, self.g.at[half, j, r], self.sent.at[j], sem, device_id={"tp": to}, device_id_type=pl.DeviceIdType.MESH
         ).start()
 
-    def wait(self, sem, shards, rows):
-        ref = self.g.at[pl.ds(0, shards), pl.ds(0, rows), pl.ds(0, self.c)]
+    def wait(self, sem, shards):
+        ref = self.own_ref.at[:, pl.ds(0, shards * C)]
         pltpu.make_async_copy(ref, ref, sem).wait()
 
+    def own(self, j):
+        return self.own_ref.at[:, pl.ds(pl.multiple_of(j * C, C), C)]
+
     def first(self, j):
-        for q in range(3):
-            m = masks(j + q)
-            for phase in range(3):
-                self.send(j, q, self.me, across(self.me, m[phase]), phase, self.own_ref)
-            self.send(j, q, self.me, across(self.me, 1), 3, self.own_ref)
+        m = masks(j)
+        for phase in range(3):
+            self.send(j, self.own(j), 0, 2**phase, across(self.me, m[phase]), self.arrived.at[phase, j])
+        self.send(j, self.own(j), 1, 0, across(self.me, 1), self.paired.at[j])
 
     def forward(self, phase, j):
-        for q in range(3):
-            self.wait(self.arrived.at[phase, 3 * j + q], 2**phase, PIECES[q][1])
-            m = masks(j + q)
-            shards = [across(self.me, m[phase])]
-            for earlier in range(phase):
-                shards += [across(s, m[earlier]) for s in shards]
-            for s in shards:
-                for later in range(phase + 1, 3):
-                    self.send(j, q, s, across(self.me, m[later]), later)
-                self.send(j, q, s, across(self.me, 1), 3)
+        self.wait(self.arrived.at[phase, j], 2**phase)
+        m = masks(j)
+        if phase == 0:
+            for later in (1, 2):
+                self.send(j, self.g.at[0, j, 1], 0, 1 + 2**later, across(self.me, m[later]), self.arrived.at[later, j])
+        elif phase == 1:
+            self.send(j, self.g.at[0, j, pl.ds(2, 2)], 0, pl.ds(6, 2), across(self.me, m[2]), self.arrived.at[2, j])
+        else:
+            self.send(j, self.g.at[0, j, pl.ds(1, 7)], 1, pl.ds(1, 7), across(self.me, 1), self.paired.at[j])
+
+    def copies(self, j, dst, sem):
+        m = masks(j)
+        out = []
+        for half in range(2):
+            for r in range(8):
+                device, block = across(self.me, 1) if half else self.me, jnp.int32(8 * half)
+                for k in range(3):
+                    if r & (1 << k):
+                        device, block = across(device, m[k]), block + lax.div(m[k], jnp.int32(2))
+                at = pl.multiple_of((block if self.relative else device) * SHARD, SHARD)
+                src = self.g.at[half, j, r] if half or r else self.own(j)
+                out.append(pltpu.make_async_copy(src, dst(pl.ds(at, SHARD)), sem))
+        return out
 
     def load(self, j):
-        self.wait(self.paired.at[j], 8, SHARD)
-        slot = lax.rem(j, 2)
-        for r in range(N):
-            device, at = self.place(r)
-            src = self.own_ref.at[:, self.cols(j)] if r == 0 else self.g.at[device, :, self.cols(j)]
-            dst = self.buf.at[slot, pl.ds(pl.multiple_of(at * SHARD, SHARD), SHARD)]
-            pltpu.make_async_copy(src, dst, self.loaded.at[slot]).start()
+        self.wait(self.paired.at[j], 8)
+        slot = lax.rem(lax.div(j, jnp.int32(self.width)), 2)
+        cols = pl.ds(pl.multiple_of(lax.rem(j, jnp.int32(self.width)) * C, C), C)
+        for c in self.copies(j, lambda rows: self.buf.at[slot, rows, cols], self.loaded.at[slot]):
+            c.start()
 
     def guarded(self, j, f):
-        @pl.when((j >= 0) & (j < self.chunks))
+        @pl.when((j >= 0) & (j < self.CHUNKS))
         def _():
             f(j)
 
@@ -118,7 +126,7 @@
         return slot
 
     def finish(self):
-        loop(0, self.chunks, lambda j: self.wait(self.sent.at[j], 15, SHARD))
+        loop(0, self.CHUNKS, lambda j: self.wait(self.sent.at[j], 15))
 
 
 def wait_like(ref, sem):
@@ -133,27 +141,23 @@
     return device
 
 
-def kernel(*refs):
+def main_kernel(*refs):
     it = iter(refs)
     take = lambda n: [next(it) for _ in range(n)]
     x, dy, gate, up, w_gate, w_up, w_down = take(7)
-    dx, dwg, dwu, dwd, gy, gx, pair, l1, l2, l3 = take(10)
+    dx, dwg, dwu, dwd, d_out, gy, gx, pair, l1, l2, l3 = take(11)
     d, acc, ht, ybuf, wd, o, kept = take(7)
     w, xbuf, sa, sb, sc, sd, se, ab, ac, ad, ae = take(11)
     y_sems, x_sems = take(4), take(4)
-    wd_sem, o_sem, kept_sem, ox_sem = take(4)
+    wd_sem, o_sem, kept_sem, ox_sem, d_sem = take(5)
     w_sem, pair_sem, r1, r2, r3, send_sem, load_sem, out_sem = take(8)
     me = lax.axis_index("tp").astype(jnp.int32)
     partner = across(me, 1)
 
-    def absolute(r):
-        s = lax.rem(me + r, jnp.int32(N))
-        return s, s
-
-    y = Gather(dy, gy, ybuf, CY, (4, 3, 2, 7), absolute, *y_sems)
-    xg = Gather(x, gx, xbuf, CX, LEADS_X, lambda p: (relative(me, p), p), *x_sems)
-
-    for j in range(3):
+    y = Gather(dy, gy, ybuf, LEADS_Y, False, *y_sems)
+    xg = Gather(x, gx, xbuf, LEADS_X, True, *x_sems)
+
+    for j in range(LEADS_Y[3] - TILES):
         y.first(jnp.int32(j))
 
     def fetch(slot, start, rows):
@@ -165,12 +169,19 @@
         wait_like(kept.at[slot, :, pl.ds(0, rows)], kept_sem.at[slot])
         return [kept[slot, k, :rows].astype(F32) for k in range(2)]
 
+    def wide(j):
+        return pl.ds(pl.multiple_of(j * CW, CW), CW)
+
     def wd_fetch(j):
         slot = lax.rem(j, 2)
-        pltpu.make_async_copy(w_down.at[:, y.cols(j)], wd.at[slot], wd_sem.at[slot]).start()
+        pltpu.make_async_copy(w_down.at[:, wide(j)], wd.at[slot], wd_sem.at[slot]).start()
 
     fetch(0, 0, T)
     wd_fetch(jnp.int32(0))
+
+    def pump_y(t):
+        y.guarded(t + 2, y.load)
+        y.pump(t)
 
     def hide(i):
         slot, rows = lax.rem(i, 2), pl.ds(pl.multiple_of(i * T, T), T)
@@ -183,17 +194,12 @@
         ht[:, rows] = (gt * jax.nn.sigmoid(gt) * ut).T.astype(BF)
         acc[rows, :] = jnp.zeros((T, F), F32)
 
-        @pl.when((lax.rem(i, 2) == 1) & (i < 8))
-        def _():
-            t = lax.div(i, 2) - 4
-            y.guarded(t + 1, y.load)
-            y.pump(t)
+        pump_y(i - TILES)
 
     loop(0, TILES, hide)
 
     def chunk(j):
-        y.guarded(j + 1, y.load)
-        y.pump(j)
+        pump_y(2 * j)
 
         @pl.when(j >= X_FROM)
         def _():
@@ -212,13 +218,14 @@
             acc[rows, :] += dot(ybuf[slot, rows, :], wd[slot], NT)
 
         loop(0, 2, rows_of)
+        pump_y(2 * j + 1)
 
         @pl.when(j >= 2)
         def _():
             wait_like(o.at[slot], o_sem.at[slot])
 
         o[slot] = dot(ht[...], ybuf[slot]).astype(BF)
-        pltpu.make_async_copy(o.at[slot], dwd.at[:, y.cols(j)], o_sem.at[slot]).start()
+        pltpu.make_async_copy(o.at[slot], dwd.at[:, wide(j)], o_sem.at[slot]).start()
 
     loop(0, CHUNKS, chunk)
 
@@ -236,6 +243,7 @@
         if p % 3 == 2:
             xg.pump(jnp.int32(sent_x + p // 3))
     pumped = sent_x + N // 3
+    pltpu.make_async_copy(d, d_out, d_sem).start()
 
     def w_start(t):
         rows, slot = pl.ds(pl.multiple_of(t * E, E), E), lax.rem(t, 3)
@@ -335,7 +343,15 @@
             se[slot] = v.astype(BF)
             pltpu.make_async_copy(se.at[slot], dx.at[:, pl.ds(pl.multiple_of(u * E, E), E)], out_sem.at[slot]).start()
 
-        def weights(u, m, r):
+        def due(t, f):
+            last = lax.div(t, jnp.int32(STEPS))
+            u = t - LAG_X + last * (EARLY - HELD - STEPS + LAG_X)
+
+            @pl.when((u >= 0) & (u < EARLY - HELD * (1 - last)))
+            def _():
+                f(u)
+
+        def weights(u):
             slot = xg.held(u)
 
             @pl.when(u >= 2)
@@ -343,7 +359,7 @@
                 wait_like(kept.at[slot], ox_sem.at[slot])
 
             v = dot(xbuf[slot], d[...], TN)
-            rows = pl.ds(pl.multiple_of(u * CX, CX), CX)
+            rows = pl.ds(pl.multiple_of(u * C, C), C)
             for k, ref in enumerate((dwg, dwu)):
                 kept[slot, k] = v[:, k * F : (k + 1) * F].astype(BF)
                 pltpu.make_async_copy(kept.at[slot, k], ref.at[rows], ox_sem.at[slot]).start()
@@ -352,7 +368,7 @@
         def _():
             w_start(t + 1)
 
-        at(LAG_X - 1, lambda u, m, r: xg.load(u))
+        due(t + 1, xg.load)
         at(LAG_B, get_b)
         at(LAG_C, get_c)
         at(LAG_D, get_d)
@@ -363,60 +379,174 @@
         at(LAG_D, stage_d)
         at(LAG_E, stage_e)
         xg.pump(t + pumped)
-        at(LAG_X, weights)
+        due(t, weights)
 
     w_start(jnp.int32(0))
-    loop(0, STEPS + max(LAG_E, LAG_X), step)
+    loop(0, STEPS + LAG_E, step)
     for slot in range(2):
         for stage, ref in enumerate((sa, sb, sc, sd)):
             wait_like(ref.at[slot], send_sem.at[stage, slot])
         wait_like(se.at[slot], out_sem.at[slot])
         wait_like(o.at[slot], o_sem.at[slot])
         wait_like(kept.at[slot], ox_sem.at[slot])
+    loop(EARLY, xg.CHUNKS, lambda j: xg.wait(xg.paired.at[j], 8))
+    wait_like(d, d_sem)
     y.finish()
     xg.finish()
+
+
+def last_kernel(*refs):
+    it = iter(refs)
+    take = lambda n: [next(it) for _ in range(n)]
+    x, gx, d_in, dx_in, *finished = take(7)
+    dx, *outs = take(4)
+    d, xbuf, o, dxbuf, *bufs = take(7)
+    d_sem, x_sem, o_sem, dx_sem, in_sem, out_sem = take(6)
+
+    xg = Gather(x, gx, xbuf, None, True, None, None, None, None)
+
+    def load(u):
+        slot = lax.rem(u, 2)
+        for c in xg.copies(EARLY + u, lambda rows: xbuf.at[slot, rows], x_sem.at[slot]):
+            c.start()
+
+    def piece(buf, u):
+        rows = buf.shape[1]
+        return pl.ds(pl.multiple_of(u * rows, rows), rows)
+
+    def bring(u):
+        for k in range(3):
+            slot = lax.rem(u, 3)
+            src = finished[k].at[piece(bufs[k], u)]
+            pltpu.make_async_copy(src, bufs[k].at[slot], in_sem.at[k, slot]).start()
+
+    pltpu.make_async_copy(d_in, d, d_sem).start()
+    load(jnp.int32(0))
+    pltpu.make_async_copy(dx_in, dxbuf, dx_sem).start()
+    bring(jnp.int32(0))
+    bring(jnp.int32(1))
+    wait_like(d, d_sem)
+
+    def step(u):
+        slot, ring = lax.rem(u, 2), lax.rem(u, 3)
+
+        @pl.when(u + 1 < LATE)
+        def _():
+            load(u + 1)
+
+        for k in range(3):
+            wait_like(bufs[k].at[ring], in_sem.at[k, ring])
+            pltpu.make_async_copy(bufs[k].at[ring], outs[k].at[piece(bufs[k], u)], out_sem.at[k, ring]).start()
+
+        @pl.when(u >= 1)
+        def _():
+            before = lax.rem(u + 2, 3)
+            for k in range(3):
+                wait_like(bufs[k].at[before], out_sem.at[k, before])
+
+        @pl.when(u + 2 < LATE)
+        def _():
+            bring(u + 2)
+
+        @pl.when(u == 1)
+        def _():
+            wait_like(dxbuf, dx_sem)
+            pltpu.make_async_copy(dxbuf, dx, dx_sem).start()
+
+        wait_like(xbuf.at[slot], x_sem.at[slot])
+
+        @pl.when(u >= 2)
+        def _():
+            wait_like(o.at[slot], o_sem.at[slot])
+
+        v = dot(xbuf[slot], d[...], TN)
+        rows = pl.ds(pl.multiple_of((EARLY + u) * C, C), C)
+        for k in range(2):
+            o[slot, k] = v[:, k * F : (k + 1) * F].astype(BF)
+            pltpu.make_async_copy(o.at[slot, k], outs[k].at[rows], o_sem.at[slot]).start()
+
+    loop(0, LATE, step)
+    for k in range(3):
+        wait_like(bufs[k].at[(LATE - 1) % 3], out_sem.at[k, (LATE - 1) % 3])
+    for slot in range(2):
+        wait_like(o.at[slot], o_sem.at[slot])
+    wait_like(dxbuf, dx_sem)
 
 
 def solution(mesh):
     sds, vmem = jax.ShapeDtypeStruct, lambda *s: pltpu.VMEM(s, BF)
     dma = pltpu.SemaphoreType.DMA
 
-    def step(*args):
-        outs = [sds((SHARD, D), BF), sds((D, F), BF), sds((D, F), BF), sds((F, D), BF)]
-        outs += [sds((N, SHARD, D), BF)] * 2
-        outs += [sds((STEPS, ROWS // 2, E), BF)] + [sds((STEPS, n, SHARD, E), BF) for n in (4, 2, 1)]
+    def call(kernel, outs, scratch, products, args, **params):
         return pl.pallas_call(
             kernel,
             out_shape=outs,
             in_specs=[ANY] * len(args),
             out_specs=[ANY] * len(outs),
-            scratch_shapes=[
+            scratch_shapes=scratch,
+            cost_estimate=pl.CostEstimate(flops=products * ROWS * D * F, bytes_accessed=2**28, transcendentals=0),
+            compiler_params=pltpu.CompilerParams(vmem_limit_bytes=63 * 2**20, **params),
+        )(*args)
+
+    def step(x, dy, gate, up, w_gate, w_up, w_down):
+        early = EARLY * C
+        dx, dwg, dwu, dwd, d, _, gx, *_ = call(
+            main_kernel,
+            [sds((SHARD, D), BF), sds((early, F), BF), sds((early, F), BF), sds((F, D), BF), sds((ROWS, 2 * F), BF)]
+            + [sds((2, D // C, 8, SHARD, C), BF)] * 2
+            + [sds((STEPS, ROWS // 2, E), BF)]
+            + [sds((STEPS, n, SHARD, E), BF) for n in (4, 2, 1)],
+            [
                 vmem(ROWS, 2 * F),
                 pltpu.VMEM((ROWS, F), F32),
                 vmem(F, ROWS),
-                vmem(2, ROWS, CY),
-                vmem(2, F, CY),
-                vmem(2, F, CY),
+                vmem(2, ROWS, CW),
+                vmem(2, F, CW),
+                vmem(2, F, CW),
                 vmem(2, 2, T, F),
                 vmem(3, E, 2 * F),
-                vmem(2, ROWS, CX),
+                vmem(2, ROWS, C),
                 vmem(2, ROWS // 2, E),
                 *[vmem(2, n, SHARD, E) for n in (4, 2, 1)],
                 vmem(2, SHARD, E),
                 vmem(ROWS // 2, E),
                 *[vmem(n, SHARD, E) for n in (2, 2, 3)],
-                *Gather.sems(CY),
-                *Gather.sems(CX),
+                *Gather.SEMS,
+                *Gather.SEMS,
                 *[dma((2,))] * 4,
+                dma,
                 dma((3,)),
                 *[dma((STEPS,))] * 4,
                 dma((4, 2)),
                 dma((4,)),
                 dma((2,)),
             ],
-            cost_estimate=pl.CostEstimate(flops=12 * ROWS * D * F, bytes_accessed=400 * 2**20, transcendentals=0),
-            compiler_params=pltpu.CompilerParams(has_side_effects=True, vmem_limit_bytes=63 * 2**20),
-        )(*args)[:4]
+            11,
+            (x, dy, gate, up, w_gate, w_up, w_down),
+            has_side_effects=True,
+        )
+        dx, dwg, dwu, dwd = call(
+            last_kernel,
+            [sds((SHARD, D), BF), sds((D, F), BF), sds((D, F), BF), sds((F, D), BF)],
+            [
+                vmem(ROWS, 2 * F),
+                vmem(2, ROWS, C),
+                vmem(2, 2, C, F),
+                vmem(SHARD, D),
+                vmem(3, early // LATE, F),
+                vmem(3, early // LATE, F),
+                vmem(3, F // LATE, D),
+                dma,
+                dma((2,)),
+                dma((2,)),
+                dma,
+                dma((3, 3)),
+                dma((3, 3)),
+            ],
+            1,
+            (x, gx, d, dx, dwg, dwu, dwd),
+        )
+        return dx, dwg, dwu, dwd
 
     rows, cols = P(("dp", "tp"), None), P("dp", "tp")
     weight, down = P(None, "tp"), P("tp", None)

time: 458 us -> 442 us (0.965)
  local copies, waits for them, and re-layouts: 36.7 us -> 0 us
  Pallas kernels: 419 us -> 440 us
    unnamed x14 -> x0, local copies, waits for them, and re-layouts: 36.7 us -> none
    pallas_call x1 -> x2, Pallas kernels: 419 us -> 440 us  [call(): pl.pallas_call(kernel, out_shape=outs, in_specs=[ANY] * len(args), out_sp...]
where the time goes in v3:
time: 442 us; the launch traced here: 441 us
  Pallas kernels  440 us (100%)
    pallas_call x2, Pallas kernels, call(): pl.pallas_call(kernel, out_shape=outs, in_specs=[ANY] * len(args), out_sp...  440 us

profile of v3, /device:TPU:0, one launch (start us, length us, event | category | flops | bytes accessed | tf_op | source)
XLA Modules:
  0.0 440.8 jit_solution(12487382475618875423)
XLA Ops:
  0.6 400.2 %shard_map.102 = (bf16[160,7168]{1,0:T(8,128)(2,1)}, bf16[5120,1152]{1,0:T(8,128)(2,1)}, bf16[5120,1152]{1,0:T(8,128)(2,1)}, bf16[1152,7168]{1,0:T(8,128)(2,1)},...) custom-call(bf16[160,7168]{1,0:T(8,128)(2,1)} %refs_0_.3, ...), custom_call_target="tpu_custom_call" | custom-call | flops 232532213760 | bytes 268435456 | tf_op jit(solution)/shard_map/pallas_call | solution.py:481
  400.8 39.9 %shard_map.103 = (bf16[160,7168]{1,0:T(8,128)(2,1)}, bf16[7168,1152]{1,0:T(8,128)(2,1)}, bf16[7168,1152]{1,0:T(8,128)(2,1)}, bf16[1152,7168]{1,0:T(8,128)(2,1)}) custom-call(bf16[160,7168]{1,0:T(8,128)(2,1)} %refs_0_.3, bf16[2,28,8,160,256]{4,3,2,1,0:T(8,128)(2,1)} %get-tuple-element.10.refs_1_, bf16[2560,2304]{1,0:T(8,128)(2,1)} %get-tuple-element.11.refs_2_, ...), custom_call_target="tpu_custom_call" | custom-call | flops 21139292160 | bytes 268435456 | tf_op jit(solution)/shard_map/pallas_call | solution.py:481
